TPU v7x, 512 devices: a whole 4x4x16 slice. The times are simulated.
512 devices in a mesh: group: 4 (over z_hi, core), gx: 32 (over z_lo, y), gy: 4 (over x).
Axes of the slice: x: 4, y: 4, z: 16 (z_hi: 2, z_lo: 8; z = z_hi * 8 + z_lo), core: 2. Of those that a mesh axis runs over, the one named last changes fastest.
Arguments:
- parent_mass: float32 [512, 512, 512], P('gx', ('group', 'gy')), may hold values from -6 to 6
- fine_mass: float32 [512, 128, 128], P('gx', ('group', 'gy')), may hold values from -6 to 6
- offsets: int32 [3], replicated, may hold values from 0 to 511
Outputs:
- parent_potential: float32 [512, 512, 512], P('gx', ('group', 'gy'))
- fine_potential: float32 [512, 128, 128], P('gx', ('group', 'gy'))
All inputs are finite; a program needn't handle non-finite values.
Results may differ from a plain program's by a relative error of at most 0.0003.
Values sent between devices are 32-bit elements; how exact they have to be, the bound alone decides.
No kernel may reach another device: no remote copies, remote signals or barrier semaphores. Data moves between devices by JAX's collectives and lax.ppermute only.
A program may use at most 128 MiB of HBM per device.

v0:
```python
import math

import jax
import jax.numpy as jnp
from jax import lax
from jax.sharding import PartitionSpec as P

NP = 512
CYCLES = 2
LEVELS = 3
SWEEPS = 2
COARSE_SWEEPS = 4


OMEGA = 6.0 / 7.0
HIGH = lax.Precision.HIGHEST


def extended(shard, sides, width):
    edges = {}
    for axis, dim in sides:
        size, length = (lax.axis_size(axis), shard.shape[dim])
        up = [(i, (i + 1) % size) for i in range(size - 1)]
        last = lax.slice_in_dim(shard, length - width, length, axis=dim)
        initial = lax.slice_in_dim(shard, 0, width, axis=dim)
        edges[dim] = (
            lax.ppermute(last, axis, up),
            lax.ppermute(initial, axis, [(b, a) for a, b in up]),
        )
    done = []
    for _, dim in sides:
        low, high = edges[dim]
        around = [(width, width) if d in done else (0, 0) for d in range(shard.ndim)]
        shard = jnp.concatenate([jnp.pad(low, around), shard, jnp.pad(high, around)], axis=dim)
        done.append(dim)
    return shard


def cas_table(wave, places, length):
    phase = wave[:, None] * places[None, :] % length
    angle = phase.astype(jnp.float32) * (2.0 * math.pi / length)
    return jnp.cos(angle) + jnp.sin(angle)


def eigen_of(wave, length):
    sine = jnp.sin(wave.astype(jnp.float32) * (math.pi / length))
    return 4.0 * sine * sine


def green(wave_a, wave_b, wave_c):
    lam = (
        eigen_of(wave_a, NP)[:, None, None]
        + eigen_of(wave_b, NP)[None, :, None]
        + eigen_of(wave_c, NP)[None, None, :]
    )
    inverse = jnp.where(lam > 0, 1.0 / jnp.where(lam > 0, lam, 1.0), 0.0)
    return inverse * (1.0 / float(NP**3))


def last_axis(block, table):
    return jnp.einsum("abj,kj->abk", block, table, precision=HIGH)


def middle_axis(block, table):
    return jnp.einsum("ajc,kj->akc", block, table, precision=HIGH)


def first_axis(block, table):
    product = jnp.dot(table, block.reshape(block.shape[0], -1), precision=HIGH)
    return product.reshape((table.shape[0],) + block.shape[1:])


def coarsen(block):
    a, b, c = block.shape
    return block.reshape(a // 2, 2, b // 2, 2, c // 2, 2).sum(axis=(1, 3, 5))


def refine(block):
    return jnp.repeat(jnp.repeat(jnp.repeat(block, 2, axis=0), 2, axis=1), 2, axis=2)


def stencil(field, padded):
    beside = padded[2:, 1:-1, 1:-1] + padded[:-2, 1:-1, 1:-1]
    beside = beside + padded[1:-1, 2:, 1:-1] + padded[1:-1, :-2, 1:-1]
    beside = beside + padded[1:-1, 1:-1, 2:] + padded[1:-1, 1:-1, :-2]
    return 6.0 * field - beside


def operate(field, edge, flags):
    padded = extended(field, (("gx", 0), (("group", "gy"), 1)), 1)
    if edge:
        padded = padded.at[0, 1:-1].set(jnp.where(flags[0], field[0], padded[0, 1:-1]))
        padded = padded.at[-1, 1:-1].set(jnp.where(flags[1], field[-1], padded[-1, 1:-1]))
        padded = padded.at[1:-1, 0].set(jnp.where(flags[2], field[:, 0], padded[1:-1, 0]))
        padded = padded.at[1:-1, -1].set(jnp.where(flags[3], field[:, -1], padded[1:-1, -1]))
        padded = jnp.pad(padded, ((0, 0), (0, 0), (1, 1)), mode="edge")
    else:
        padded = jnp.pad(padded, ((0, 0), (0, 0), (1, 1)))
    return stencil(field, padded)


def smooth(corr, resid, sweeps, flags):
    for turn in range(sweeps):
        if corr is None:
            corr = OMEGA / 6.0 * resid
        else:
            corr = corr + OMEGA / 6.0 * (resid - operate(corr, False, flags))
    return corr


def coarsest(resid, flags):
    return smooth(None, resid, COARSE_SWEEPS, flags)


def cycle(corr, resid, level, flags, index_x, index_y):
    if level == LEVELS - 1:
        return coarsest(resid, flags)
    corr = smooth(corr, resid, SWEEPS, flags)
    lower = 0.5 * coarsen(resid - operate(corr, False, flags))
    below = cycle(None, lower, level + 1, flags, index_x, index_y)
    corr = corr + refine(below)
    return smooth(corr, resid, SWEEPS, flags)


def local(parent_mass, fine_mass, offsets):
    count_x = lax.axis_size("gx")
    count_y = lax.axis_size(("group", "gy"))
    index_x = lax.axis_index("gx")
    index_y = lax.axis_index(("group", "gy"))
    wave = jnp.arange(NP, dtype=jnp.int32)
    full = cas_table(wave, wave, NP)
    rest = coarsen(fine_mass)
    span_x = rest.shape[0] * count_x
    span_y = rest.shape[1] * count_y
    x_table = cas_table(wave, offsets[0] + jnp.arange(span_x, dtype=jnp.int32), NP)
    y_table = cas_table(wave, offsets[1] + jnp.arange(span_y, dtype=jnp.int32), NP)
    z_table = cas_table(wave, offsets[2] + jnp.arange(rest.shape[2], dtype=jnp.int32), NP)
    dense = last_axis(parent_mass, full)
    light = last_axis(rest, z_table)
    dense, light = (
        lax.all_to_all(dense, "gx", split_axis=2, concat_axis=0, tiled=True),
        lax.all_to_all(light, "gx", split_axis=2, concat_axis=0, tiled=True),
    )
    dense = first_axis(dense, full)
    light = first_axis(light, x_table)
    dense, light = (
        lax.all_to_all(dense, ("group", "gy"), split_axis=0, concat_axis=1, tiled=True),
        lax.all_to_all(light, ("group", "gy"), split_axis=0, concat_axis=1, tiled=True),
    )
    spectrum = middle_axis(dense, full) + middle_axis(light, y_table)
    width_a = spectrum.shape[0]
    width_c = spectrum.shape[2]
    spectrum = spectrum * green(
        index_y * width_a + jnp.arange(width_a, dtype=jnp.int32),
        wave,
        index_x * width_c + jnp.arange(width_c, dtype=jnp.int32),
    )
    whole = middle_axis(spectrum, full)
    near = middle_axis(spectrum, y_table.T)
    whole, near = (
        lax.all_to_all(whole, ("group", "gy"), split_axis=1, concat_axis=0, tiled=True),
        lax.all_to_all(near, ("group", "gy"), split_axis=1, concat_axis=0, tiled=True),
    )
    whole = first_axis(whole, full)
    near = first_axis(near, x_table.T)
    whole, near = (
        lax.all_to_all(whole, "gx", split_axis=0, concat_axis=2, tiled=True),
        lax.all_to_all(near, "gx", split_axis=0, concat_axis=2, tiled=True),
    )
    potential = last_axis(whole, full)
    footprint = last_axis(near, z_table.T)
    flags = (index_x == 0, index_x == count_x - 1, index_y == 0, index_y == count_y - 1)
    start = refine(footprint)
    resid = 2.0 * fine_mass - operate(start, True, flags)
    corr = None
    for turn in range(CYCLES):
        corr = cycle(corr, resid, 0, flags, index_x, index_y)
    return (potential, start + corr)


def solution(mesh):
    return jax.shard_map(
        local,
        mesh=mesh,
        in_specs=(P("gx", ("group", "gy"), None), P("gx", ("group", "gy"), None), P()),
        out_specs=(P("gx", ("group", "gy"), None), P("gx", ("group", "gy"), None)),
        check_vma=False,
    )
```

profile of v0, /device:TPU:135, one launch (start us, length us, event | category | flops | bytes accessed | tf_op | source)
XLA Modules:
  0.0 1044.9 jit_solution(9459610186346306558)
XLA Ops:
  0.7 6.4 reshape.326
  13.9 13.5 %all-to-all-start.2 = ((f32[32,1,512]{2,1,0:T(1,128)}), f32[32,1,512]{2,1,0:T(1,128)S(1)}, u32[]{:S(2)}, u32[]{:S(2)}) async-start(f32[32,1,512]{2,1,0:T(1,128)} %reshape.359), calls=%async_computation.2 | async-start | bytes 131072 | tf_op jit(solution)/shard_map/all_to_all | solution.py:142
  27.4 6.7 convolution_bitcast_fusion.1
  42.5 12.3 %all-to-all-start = ((f32[32,1,8192]{2,1,0:T(1,128)}), f32[32,1,8192]{2,1,0:T(1,128)S(1)}, u32[]{:S(2)}, u32[]{:S(2)}) async-start(f32[32,1,8192]{2,1,0:T(1,128)} %reshape.355), calls=%async_computation | async-start | bytes 2097152 | tf_op jit(solution)/shard_map/all_to_all | solution.py:141
  63.8 37.1 %all-to-all-done = f32[32,1,8192]{2,1,0:T(1,128)S(1)} async-done(((f32[32,1,8192]{2,1,0:T(1,128)}), f32[32,1,8192]{2,1,0:T(1,128)S(1)}, u32[]{:S(2)}, u32[]{:S(2)}) %all-to-all-start) | async-done | bytes 1048608 | tf_op jit(solution)/shard_map/all_to_all | solution.py:141
  100.9 11.4 %all-to-all-start.3 = ((f32[16,1,2048]{2,1,0:T(1,128)}), f32[16,1,2048]{2,1,0:T(1,128)S(1)}, u32[]{:S(2)}, u32[]{:S(2)}) async-start(f32[16,1,2048]{2,1,0:T(1,128)} %reshape.361), calls=%async_computation.3 | async-start | bytes 262144 | tf_op jit(solution)/shard_map/all_to_all | solution.py:148
  118.4 7.0 copy.590
  125.4 7.8 reshape.325
  133.5 6.4 fusion.15
  148.3 14.9 %all-to-all-start.1 = ((f32[16,1,16384]{2,1,0:T(1,128)}), f32[16,1,16384]{2,1,0:T(1,128)S(1)}, u32[]{:S(2)}, u32[]{:S(2)}) async-start(f32[16,1,16384]{2,1,0:T(1,128)} %reshape.357), calls=%async_computation.1 | async-start | bytes 2097152 | tf_op jit(solution)/shard_map/all_to_all | solution.py:147
  167.1 50.5 %all-to-all-done.1 = f32[16,1,16384]{2,1,0:T(1,128)S(1)} async-done(((f32[16,1,16384]{2,1,0:T(1,128)}), f32[16,1,16384]{2,1,0:T(1,128)S(1)}, u32[]{:S(2)}, u32[]{:S(2)}) %all-to-all-start.1) | async-done | bytes 1048608 | tf_op jit(solution)/shard_map/all_to_all | solution.py:147
  223.6 6.6 copy.655
  233.8 6.8 fusion.13
  244.6 18.9 %all_to_all.132 = f32[16,1,2048]{2,1,0:T(1,128)S(1)} all-to-all(f32[16,1,2048]{2,1,0:T(1,128)S(1)} %reshape.367), channel_id=1, replica_groups=mesh['group'=4,'gx'=32,'gy'=4] {'group','gy'}, dimensions={0} | all-to-all | bytes 262144 | tf_op jit(solution)/shard_map/all_to_all | solution.py:162
  269.1 12.2 %all-to-all-start.7 = ((f32[32,1,512]{2,1,0:T(1,128)}), f32[32,1,512]{2,1,0:T(1,128)S(1)}, u32[]{:S(2)}, u32[]{:S(2)}) async-start(f32[32,1,512]{2,1,0:T(1,128)} %reshape.369), calls=%async_computation.7 | async-start | bytes 131072 | tf_op jit(solution)/shard_map/all_to_all | solution.py:168
  281.9 6.4 all-to-all-done.7
  296.5 13.6 %collective-permute-start = (f32[16,1,128]{2,1,0:T(1,128)S(1)}, f32[16,1,128]{2,1,0:T(1,128)S(1)}, u32[]{:S(2)}, u32[]{:S(2)}) collective-permute-start(f32[16,1,128]{2,1,0:T(1,128)S(1)} %get-tuple-element.98), channel_id=1, source_target_pairs={{0,1},{1,2},{2,3},{3,128},{128,129},{129,130},{130,131},{131,256},... | collective-permute-start | bytes 24584 | tf_op jit(solution)/shard_map/ppermute | solution.py:27
  310.2 6.4 collective-permute-start.2
  321.3 14.5 %collective-permute-start.7 = (f32[16,1,128]{2,1,0:T(1,128)S(1)}, f32[16,1,128]{2,1,0:T(1,128)S(1)}, u32[]{:S(2)}, u32[]{:S(2)}) collective-permute-start(f32[16,1,128]{2,1,0:T(1,128)S(1)} %get-tuple-element.96), channel_id=1, source_target_pairs={{0,1},{1,2},{2,3},{3,128},{128,129},{129,130},{130,131},{131,256},... | collective-permute-start | bytes 24584 | tf_op jit(solution)/shard_map/ppermute | solution.py:27
  335.8 6.9 collective-permute-start.4
  352.7 14.5 %collective-permute-start.11 = (f32[16,1,128]{2,1,0:T(1,128)S(1)}, f32[16,1,128]{2,1,0:T(1,128)S(1)}, u32[]{:S(2)}, u32[]{:S(2)}) collective-permute-start(f32[16,1,128]{2,1,0:T(1,128)S(1)} %get-tuple-element.92), channel_id=1, source_target_pairs={{0,1},{1,2},{2,3},{3,128},{128,129},{129,130},{130,131},{131,256},... | collective-permute-start | bytes 24584 | tf_op jit(solution)/shard_map/ppermute | solution.py:27
  387.4 14.5 %collective-permute-start.15 = (f32[8,1,64]{2,1,0:T(1,128)S(1)}, f32[8,1,64]{2,1,0:T(1,128)S(1)}, u32[]{:S(2)}, u32[]{:S(2)}) collective-permute-start(f32[8,1,64]{2,1,0:T(1,128)S(1)} %get-tuple-element.132), channel_id=1, source_target_pairs={{0,1},{1,2},{2,3},{3,128},{128,129},{129,130},{130,131},{131,256},... | collective-permute-start | bytes 6152 | tf_op jit(solution)/shard_map/ppermute | solution.py:27
  413.6 14.5 %collective-permute-start.19 = (f32[8,1,64]{2,1,0:T(1,128)S(1)}, f32[8,1,64]{2,1,0:T(1,128)S(1)}, u32[]{:S(2)}, u32[]{:S(2)}) collective-permute-start(f32[8,1,64]{2,1,0:T(1,128)S(1)} %get-tuple-element.128), channel_id=1, source_target_pairs={{0,1},{1,2},{2,3},{3,128},{128,129},{129,130},{130,131},{131,256},... | collective-permute-start | bytes 6152 | tf_op jit(solution)/shard_map/ppermute | solution.py:27
  440.5 14.5 %collective-permute-start.23 = (f32[4,1,32]{2,0,1:T(4,128)S(1)}, f32[4,1,32]{2,0,1:T(4,128)S(1)}, u32[]{:S(2)}, u32[]{:S(2)}) collective-permute-start(f32[4,1,32]{2,0,1:T(4,128)S(1)} %get-tuple-element.156), channel_id=1, source_target_pairs={{0,1},{1,2},{2,3},{3,128},{128,129},{129,130},{130,131},{131,256},... | collective-permute-start | bytes 1544 | tf_op jit(solution)/shard_map/ppermute | solution.py:27
  466.6 14.5 %collective-permute-start.27 = (f32[4,1,32]{2,0,1:T(4,128)S(1)}, f32[4,1,32]{2,0,1:T(4,128)S(1)}, u32[]{:S(2)}, u32[]{:S(2)}) collective-permute-start(f32[4,1,32]{2,0,1:T(4,128)S(1)} %get-tuple-element.152), channel_id=1, source_target_pairs={{0,1},{1,2},{2,3},{3,128},{128,129},{129,130},{130,131},{131,256},... | collective-permute-start | bytes 1544 | tf_op jit(solution)/shard_map/ppermute | solution.py:27
  492.7 14.5 %collective-permute-start.31 = (f32[4,1,32]{2,0,1:T(4,128)S(1)}, f32[4,1,32]{2,0,1:T(4,128)S(1)}, u32[]{:S(2)}, u32[]{:S(2)}) collective-permute-start(f32[4,1,32]{2,0,1:T(4,128)S(1)} %get-tuple-element.148), channel_id=1, source_target_pairs={{0,1},{1,2},{2,3},{3,128},{128,129},{129,130},{130,131},{131,256},... | collective-permute-start | bytes 1544 | tf_op jit(solution)/shard_map/ppermute | solution.py:27
  519.2 14.5 %collective-permute-start.35 = (f32[8,1,64]{2,1,0:T(1,128)S(1)}, f32[8,1,64]{2,1,0:T(1,128)S(1)}, u32[]{:S(2)}, u32[]{:S(2)}) collective-permute-start(f32[8,1,64]{2,1,0:T(1,128)S(1)} %get-tuple-element.124), channel_id=1, source_target_pairs={{0,1},{1,2},{2,3},{3,128},{128,129},{129,130},{130,131},{131,256},... | collective-permute-start | bytes 6152 | tf_op jit(solution)/shard_map/ppermute | solution.py:27
  545.4 14.5 %collective-permute-start.39 = (f32[8,1,64]{2,1,0:T(1,128)S(1)}, f32[8,1,64]{2,1,0:T(1,128)S(1)}, u32[]{:S(2)}, u32[]{:S(2)}) collective-permute-start(f32[8,1,64]{2,1,0:T(1,128)S(1)} %get-tuple-element.120), channel_id=1, source_target_pairs={{0,1},{1,2},{2,3},{3,128},{128,129},{129,130},{130,131},{131,256},... | collective-permute-start | bytes 6152 | tf_op jit(solution)/shard_map/ppermute | solution.py:27
  572.1 14.5 %collective-permute-start.43 = (f32[16,1,128]{2,1,0:T(1,128)S(1)}, f32[16,1,128]{2,1,0:T(1,128)S(1)}, u32[]{:S(2)}, u32[]{:S(2)}) collective-permute-start(f32[16,1,128]{2,1,0:T(1,128)S(1)} %get-tuple-element.88), channel_id=1, source_target_pairs={{0,1},{1,2},{2,3},{3,128},{128,129},{129,130},{130,131},{131,256},... | collective-permute-start | bytes 24584 | tf_op jit(solution)/shard_map/ppermute | solution.py:27
  598.4 14.5 %collective-permute-start.47 = (f32[16,1,128]{2,1,0:T(1,128)S(1)}, f32[16,1,128]{2,1,0:T(1,128)S(1)}, u32[]{:S(2)}, u32[]{:S(2)}) collective-permute-start(f32[16,1,128]{2,1,0:T(1,128)S(1)} %get-tuple-element.84), channel_id=1, source_target_pairs={{0,1},{1,2},{2,3},{3,128},{128,129},{129,130},{130,131},{131,256},... | collective-permute-start | bytes 24584 | tf_op jit(solution)/shard_map/ppermute | solution.py:27
  624.8 14.5 %collective-permute-start.51 = (f32[16,1,128]{2,1,0:T(1,128)S(1)}, f32[16,1,128]{2,1,0:T(1,128)S(1)}, u32[]{:S(2)}, u32[]{:S(2)}) collective-permute-start(f32[16,1,128]{2,1,0:T(1,128)S(1)} %get-tuple-element.80), channel_id=1, source_target_pairs={{0,1},{1,2},{2,3},{3,128},{128,129},{129,130},{130,131},{131,256},... | collective-permute-start | bytes 24584 | tf_op jit(solution)/shard_map/ppermute | solution.py:27
  651.2 14.5 %collective-permute-start.55 = (f32[16,1,128]{2,1,0:T(1,128)S(1)}, f32[16,1,128]{2,1,0:T(1,128)S(1)}, u32[]{:S(2)}, u32[]{:S(2)}) collective-permute-start(f32[16,1,128]{2,1,0:T(1,128)S(1)} %get-tuple-element.76), channel_id=1, source_target_pairs={{0,1},{1,2},{2,3},{3,128},{128,129},{129,130},{130,131},{131,256},... | collective-permute-start | bytes 24584 | tf_op jit(solution)/shard_map/ppermute | solution.py:27
  671.3 6.7 convolution_bitcast_fusion
  693.6 13.9 %collective-permute-start.59 = (f32[16,1,128]{2,1,0:T(1,128)S(1)}, f32[16,1,128]{2,1,0:T(1,128)S(1)}, u32[]{:S(2)}, u32[]{:S(2)}) collective-permute-start(f32[16,1,128]{2,1,0:T(1,128)S(1)} %get-tuple-element.72), channel_id=1, source_target_pairs={{0,1},{1,2},{2,3},{3,128},{128,129},{129,130},{130,131},{131,256},... | collective-permute-start | bytes 24584 | tf_op jit(solution)/shard_map/ppermute | solution.py:27
  731.2 14.5 %collective-permute-start.63 = (f32[8,1,64]{2,1,0:T(1,128)S(1)}, f32[8,1,64]{2,1,0:T(1,128)S(1)}, u32[]{:S(2)}, u32[]{:S(2)}) collective-permute-start(f32[8,1,64]{2,1,0:T(1,128)S(1)} %get-tuple-element.116), channel_id=1, source_target_pairs={{0,1},{1,2},{2,3},{3,128},{128,129},{129,130},{130,131},{131,256},... | collective-permute-start | bytes 6152 | tf_op jit(solution)/shard_map/ppermute | solution.py:27
  751.0 10.5 %collective-permute-done.61 = f32[1,4,64]{2,1,0:T(4,128)S(1)} collective-permute-done((f32[1,4,64]{2,1,0:T(4,128)S(1)}, f32[1,4,64]{2,1,0:T(4,128)S(1)}, u32[]{:S(2)}, u32[]{:S(2)}) %collective-permute-start.61) | collective-permute-done | bytes 1056 | tf_op jit(solution)/shard_map/ppermute | solution.py:27
  763.7 14.5 %collective-permute-start.67 = (f32[8,1,64]{2,1,0:T(1,128)S(1)}, f32[8,1,64]{2,1,0:T(1,128)S(1)}, u32[]{:S(2)}, u32[]{:S(2)}) collective-permute-start(f32[8,1,64]{2,1,0:T(1,128)S(1)} %get-tuple-element.112), channel_id=1, source_target_pairs={{0,1},{1,2},{2,3},{3,128},{128,129},{129,130},{130,131},{131,256},... | collective-permute-start | bytes 6152 | tf_op jit(solution)/shard_map/ppermute | solution.py:27
  792.8 14.5 %collective-permute-start.71 = (f32[4,1,32]{2,0,1:T(4,128)S(1)}, f32[4,1,32]{2,0,1:T(4,128)S(1)}, u32[]{:S(2)}, u32[]{:S(2)}) collective-permute-start(f32[4,1,32]{2,0,1:T(4,128)S(1)} %get-tuple-element.144), channel_id=1, source_target_pairs={{0,1},{1,2},{2,3},{3,128},{128,129},{129,130},{130,131},{131,256},... | collective-permute-start | bytes 1544 | tf_op jit(solution)/shard_map/ppermute | solution.py:27
  818.9 14.5 %collective-permute-start.75 = (f32[4,1,32]{2,0,1:T(4,128)S(1)}, f32[4,1,32]{2,0,1:T(4,128)S(1)}, u32[]{:S(2)}, u32[]{:S(2)}) collective-permute-start(f32[4,1,32]{2,0,1:T(4,128)S(1)} %get-tuple-element.140), channel_id=1, source_target_pairs={{0,1},{1,2},{2,3},{3,128},{128,129},{129,130},{130,131},{131,256},... | collective-permute-start | bytes 1544 | tf_op jit(solution)/shard_map/ppermute | solution.py:27
  849.2 6.6 copy.654
  859.4 6.4 fusion.10
  874.3 8.4 all-to-all-start.5
  884.8 14.5 %collective-permute-start.79 = (f32[4,1,32]{2,0,1:T(4,128)S(1)}, f32[4,1,32]{2,0,1:T(4,128)S(1)}, u32[]{:S(2)}, u32[]{:S(2)}) collective-permute-start(f32[4,1,32]{2,0,1:T(4,128)S(1)} %get-tuple-element.136), channel_id=1, source_target_pairs={{0,1},{1,2},{2,3},{3,128},{128,129},{129,130},{130,131},{131,256},... | collective-permute-start | bytes 1544 | tf_op jit(solution)/shard_map/ppermute | solution.py:27
  913.6 14.5 %collective-permute-start.83 = (f32[8,1,64]{2,1,0:T(1,128)S(1)}, f32[8,1,64]{2,1,0:T(1,128)S(1)}, u32[]{:S(2)}, u32[]{:S(2)}) collective-permute-start(f32[8,1,64]{2,1,0:T(1,128)S(1)} %get-tuple-element.108), channel_id=1, source_target_pairs={{0,1},{1,2},{2,3},{3,128},{128,129},{129,130},{130,131},{131,256},... | collective-permute-start | bytes 6152 | tf_op jit(solution)/shard_map/ppermute | solution.py:27
  939.8 14.5 %collective-permute-start.87 = (f32[8,1,64]{2,1,0:T(1,128)S(1)}, f32[8,1,64]{2,1,0:T(1,128)S(1)}, u32[]{:S(2)}, u32[]{:S(2)}) collective-permute-start(f32[8,1,64]{2,1,0:T(1,128)S(1)} %get-tuple-element.104), channel_id=1, source_target_pairs={{0,1},{1,2},{2,3},{3,128},{128,129},{129,130},{130,131},{131,256},... | collective-permute-start | bytes 6152 | tf_op jit(solution)/shard_map/ppermute | solution.py:27
  966.5 14.5 %collective-permute-start.91 = (f32[16,1,128]{2,1,0:T(1,128)S(1)}, f32[16,1,128]{2,1,0:T(1,128)S(1)}, u32[]{:S(2)}, u32[]{:S(2)}) collective-permute-start(f32[16,1,128]{2,1,0:T(1,128)S(1)} %get-tuple-element.68), channel_id=1, source_target_pairs={{0,1},{1,2},{2,3},{3,128},{128,129},{129,130},{130,131},{131,256},... | collective-permute-start | bytes 24584 | tf_op jit(solution)/shard_map/ppermute | solution.py:27
  992.9 14.5 %collective-permute-start.95 = (f32[16,1,128]{2,1,0:T(1,128)S(1)}, f32[16,1,128]{2,1,0:T(1,128)S(1)}, u32[]{:S(2)}, u32[]{:S(2)}) collective-permute-start(f32[16,1,128]{2,1,0:T(1,128)S(1)} %get-tuple-element.64), channel_id=1, source_target_pairs={{0,1},{1,2},{2,3},{3,128},{128,129},{129,130},{130,131},{131,256},... | collective-permute-start | bytes 24584 | tf_op jit(solution)/shard_map/ppermute | solution.py:27
  1026.9 17.8 %fusion.8 = f32[16,32,512]{2,1,0:T(8,128)} fusion(f32[16,32,512]{1,2,0:T(8,128)S(1)} %bitcast.160), kind=kOutput, calls=%fused_computation.19 | convolution fusion | flops 1614544896 | bytes 2097152 | tf_op jit(solution)/shard_map/abj,kj->abk/dot_general | solution.py:61
  (449 shorter events, 400.6 us)
Async XLA Ops:
  13.9 28.6 %all-to-all-start.2 = ((f32[32,1,512]{2,1,0:T(1,128)}), f32[32,1,512]{2,1,0:T(1,128)S(1)}, u32[]{:S(2)}, u32[]{:S(2)}) async-start(f32[32,1,512]{2,1,0:T(1,128)} %reshape.359), calls=%async_computation.2 | async-start | bytes 131072 | tf_op jit(solution)/shard_map/all_to_all | solution.py:142
  42.5 58.4 %all-to-all-start = ((f32[32,1,8192]{2,1,0:T(1,128)}), f32[32,1,8192]{2,1,0:T(1,128)S(1)}, u32[]{:S(2)}, u32[]{:S(2)}) async-start(f32[32,1,8192]{2,1,0:T(1,128)} %reshape.355), calls=%async_computation | async-start | bytes 2097152 | tf_op jit(solution)/shard_map/all_to_all | solution.py:141
  100.9 47.4 %all-to-all-start.3 = ((f32[16,1,2048]{2,1,0:T(1,128)}), f32[16,1,2048]{2,1,0:T(1,128)S(1)}, u32[]{:S(2)}, u32[]{:S(2)}) async-start(f32[16,1,2048]{2,1,0:T(1,128)} %reshape.361), calls=%async_computation.3 | async-start | bytes 262144 | tf_op jit(solution)/shard_map/all_to_all | solution.py:148
  148.3 69.3 %all-to-all-start.1 = ((f32[16,1,16384]{2,1,0:T(1,128)}), f32[16,1,16384]{2,1,0:T(1,128)S(1)}, u32[]{:S(2)}, u32[]{:S(2)}) async-start(f32[16,1,16384]{2,1,0:T(1,128)} %reshape.357), calls=%async_computation.1 | async-start | bytes 2097152 | tf_op jit(solution)/shard_map/all_to_all | solution.py:147
  291.4 25.2 %collective-permute-start.1 = (f32[1,8,128]{2,1,0:T(8,128)S(1)}, f32[1,8,128]{2,1,0:T(8,128)S(1)}, u32[]{:S(2)}, u32[]{:S(2)}) collective-permute-start(f32[1,8,128]{2,1,0:T(8,128)S(1)} %copy.619), channel_id=1, source_target_pairs={{0,4},{4,8},{8,12},{12,16},{16,20},{20,24},{24,28},{28,32},{32,36}... | collective-permute-start | bytes 12296 | tf_op jit(solution)/shard_map/ppermute | solution.py:27
  293.7 23.7 %collective-permute-start.3 = (f32[16,1,128]{2,1,0:T(1,128)S(1)}, f32[16,1,128]{2,1,0:T(1,128)S(1)}, u32[]{:S(2)}, u32[]{:S(2)}) collective-permute-start(f32[16,1,128]{2,1,0:T(1,128)S(1)} %get-tuple-element.99), channel_id=1, source_target_pairs={{1,0},{2,1},{3,2},{128,3},{129,128},{130,129},{131,130},{256,131},... | collective-permute-start | bytes 24584 | tf_op jit(solution)/shard_map/ppermute | solution.py:28
  296.5 20.9 %collective-permute-start = (f32[16,1,128]{2,1,0:T(1,128)S(1)}, f32[16,1,128]{2,1,0:T(1,128)S(1)}, u32[]{:S(2)}, u32[]{:S(2)}) collective-permute-start(f32[16,1,128]{2,1,0:T(1,128)S(1)} %get-tuple-element.98), channel_id=1, source_target_pairs={{0,1},{1,2},{2,3},{3,128},{128,129},{129,130},{130,131},{131,256},... | collective-permute-start | bytes 24584 | tf_op jit(solution)/shard_map/ppermute | solution.py:27
  319.4 25.3 %collective-permute-start.6 = (f32[16,1,128]{2,1,0:T(1,128)S(1)}, f32[16,1,128]{2,1,0:T(1,128)S(1)}, u32[]{:S(2)}, u32[]{:S(2)}) collective-permute-start(f32[16,1,128]{2,1,0:T(1,128)S(1)} %get-tuple-element.97), channel_id=1, source_target_pairs={{1,0},{2,1},{3,2},{128,3},{129,128},{130,129},{131,130},{256,131},... | collective-permute-start | bytes 24584 | tf_op jit(solution)/shard_map/ppermute | solution.py:28
  321.3 23.4 %collective-permute-start.7 = (f32[16,1,128]{2,1,0:T(1,128)S(1)}, f32[16,1,128]{2,1,0:T(1,128)S(1)}, u32[]{:S(2)}, u32[]{:S(2)}) collective-permute-start(f32[16,1,128]{2,1,0:T(1,128)S(1)} %get-tuple-element.96), channel_id=1, source_target_pairs={{0,1},{1,2},{2,3},{3,128},{128,129},{129,130},{130,131},{131,256},... | collective-permute-start | bytes 24584 | tf_op jit(solution)/shard_map/ppermute | solution.py:27
  350.8 21.9 %collective-permute-start.10 = (f32[16,1,128]{2,1,0:T(1,128)S(1)}, f32[16,1,128]{2,1,0:T(1,128)S(1)}, u32[]{:S(2)}, u32[]{:S(2)}) collective-permute-start(f32[16,1,128]{2,1,0:T(1,128)S(1)} %get-tuple-element.93), channel_id=1, source_target_pairs={{1,0},{2,1},{3,2},{128,3},{129,128},{130,129},{131,130},{256,131},... | collective-permute-start | bytes 24584 | tf_op jit(solution)/shard_map/ppermute | solution.py:28
  352.7 20.0 %collective-permute-start.11 = (f32[16,1,128]{2,1,0:T(1,128)S(1)}, f32[16,1,128]{2,1,0:T(1,128)S(1)}, u32[]{:S(2)}, u32[]{:S(2)}) collective-permute-start(f32[16,1,128]{2,1,0:T(1,128)S(1)} %get-tuple-element.92), channel_id=1, source_target_pairs={{0,1},{1,2},{2,3},{3,128},{128,129},{129,130},{130,131},{131,256},... | collective-permute-start | bytes 24584 | tf_op jit(solution)/shard_map/ppermute | solution.py:27
  385.4 21.7 %collective-permute-start.14 = (f32[8,1,64]{2,1,0:T(1,128)S(1)}, f32[8,1,64]{2,1,0:T(1,128)S(1)}, u32[]{:S(2)}, u32[]{:S(2)}) collective-permute-start(f32[8,1,64]{2,1,0:T(1,128)S(1)} %get-tuple-element.133), channel_id=1, source_target_pairs={{1,0},{2,1},{3,2},{128,3},{129,128},{130,129},{131,130},{256,131},... | collective-permute-start | bytes 6152 | tf_op jit(solution)/shard_map/ppermute | solution.py:28
  411.6 21.7 %collective-permute-start.18 = (f32[8,1,64]{2,1,0:T(1,128)S(1)}, f32[8,1,64]{2,1,0:T(1,128)S(1)}, u32[]{:S(2)}, u32[]{:S(2)}) collective-permute-start(f32[8,1,64]{2,1,0:T(1,128)S(1)} %get-tuple-element.129), channel_id=1, source_target_pairs={{1,0},{2,1},{3,2},{128,3},{129,128},{130,129},{131,130},{256,131},... | collective-permute-start | bytes 6152 | tf_op jit(solution)/shard_map/ppermute | solution.py:28
  438.5 21.7 %collective-permute-start.22 = (f32[4,1,32]{2,0,1:T(4,128)S(1)}, f32[4,1,32]{2,0,1:T(4,128)S(1)}, u32[]{:S(2)}, u32[]{:S(2)}) collective-permute-start(f32[4,1,32]{2,0,1:T(4,128)S(1)} %get-tuple-element.157), channel_id=1, source_target_pairs={{1,0},{2,1},{3,2},{128,3},{129,128},{130,129},{131,130},{256,131},... | collective-permute-start | bytes 1544 | tf_op jit(solution)/shard_map/ppermute | solution.py:28
  440.5 19.8 %collective-permute-start.23 = (f32[4,1,32]{2,0,1:T(4,128)S(1)}, f32[4,1,32]{2,0,1:T(4,128)S(1)}, u32[]{:S(2)}, u32[]{:S(2)}) collective-permute-start(f32[4,1,32]{2,0,1:T(4,128)S(1)} %get-tuple-element.156), channel_id=1, source_target_pairs={{0,1},{1,2},{2,3},{3,128},{128,129},{129,130},{130,131},{131,256},... | collective-permute-start | bytes 1544 | tf_op jit(solution)/shard_map/ppermute | solution.py:27
  464.7 21.7 %collective-permute-start.26 = (f32[4,1,32]{2,0,1:T(4,128)S(1)}, f32[4,1,32]{2,0,1:T(4,128)S(1)}, u32[]{:S(2)}, u32[]{:S(2)}) collective-permute-start(f32[4,1,32]{2,0,1:T(4,128)S(1)} %get-tuple-element.153), channel_id=1, source_target_pairs={{1,0},{2,1},{3,2},{128,3},{129,128},{130,129},{131,130},{256,131},... | collective-permute-start | bytes 1544 | tf_op jit(solution)/shard_map/ppermute | solution.py:28
  466.6 19.8 %collective-permute-start.27 = (f32[4,1,32]{2,0,1:T(4,128)S(1)}, f32[4,1,32]{2,0,1:T(4,128)S(1)}, u32[]{:S(2)}, u32[]{:S(2)}) collective-permute-start(f32[4,1,32]{2,0,1:T(4,128)S(1)} %get-tuple-element.152), channel_id=1, source_target_pairs={{0,1},{1,2},{2,3},{3,128},{128,129},{129,130},{130,131},{131,256},... | collective-permute-start | bytes 1544 | tf_op jit(solution)/shard_map/ppermute | solution.py:27
  490.8 21.7 %collective-permute-start.30 = (f32[4,1,32]{2,0,1:T(4,128)S(1)}, f32[4,1,32]{2,0,1:T(4,128)S(1)}, u32[]{:S(2)}, u32[]{:S(2)}) collective-permute-start(f32[4,1,32]{2,0,1:T(4,128)S(1)} %get-tuple-element.149), channel_id=1, source_target_pairs={{1,0},{2,1},{3,2},{128,3},{129,128},{130,129},{131,130},{256,131},... | collective-permute-start | bytes 1544 | tf_op jit(solution)/shard_map/ppermute | solution.py:28
  492.7 19.8 %collective-permute-start.31 = (f32[4,1,32]{2,0,1:T(4,128)S(1)}, f32[4,1,32]{2,0,1:T(4,128)S(1)}, u32[]{:S(2)}, u32[]{:S(2)}) collective-permute-start(f32[4,1,32]{2,0,1:T(4,128)S(1)} %get-tuple-element.148), channel_id=1, source_target_pairs={{0,1},{1,2},{2,3},{3,128},{128,129},{129,130},{130,131},{131,256},... | collective-permute-start | bytes 1544 | tf_op jit(solution)/shard_map/ppermute | solution.py:27
  517.2 21.7 %collective-permute-start.34 = (f32[8,1,64]{2,1,0:T(1,128)S(1)}, f32[8,1,64]{2,1,0:T(1,128)S(1)}, u32[]{:S(2)}, u32[]{:S(2)}) collective-permute-start(f32[8,1,64]{2,1,0:T(1,128)S(1)} %get-tuple-element.125), channel_id=1, source_target_pairs={{1,0},{2,1},{3,2},{128,3},{129,128},{130,129},{131,130},{256,131},... | collective-permute-start | bytes 6152 | tf_op jit(solution)/shard_map/ppermute | solution.py:28
  543.4 21.7 %collective-permute-start.38 = (f32[8,1,64]{2,1,0:T(1,128)S(1)}, f32[8,1,64]{2,1,0:T(1,128)S(1)}, u32[]{:S(2)}, u32[]{:S(2)}) collective-permute-start(f32[8,1,64]{2,1,0:T(1,128)S(1)} %get-tuple-element.121), channel_id=1, source_target_pairs={{1,0},{2,1},{3,2},{128,3},{129,128},{130,129},{131,130},{256,131},... | collective-permute-start | bytes 6152 | tf_op jit(solution)/shard_map/ppermute | solution.py:28
  570.2 21.7 %collective-permute-start.42 = (f32[16,1,128]{2,1,0:T(1,128)S(1)}, f32[16,1,128]{2,1,0:T(1,128)S(1)}, u32[]{:S(2)}, u32[]{:S(2)}) collective-permute-start(f32[16,1,128]{2,1,0:T(1,128)S(1)} %get-tuple-element.89), channel_id=1, source_target_pairs={{1,0},{2,1},{3,2},{128,3},{129,128},{130,129},{131,130},{256,131},... | collective-permute-start | bytes 24584 | tf_op jit(solution)/shard_map/ppermute | solution.py:28
  572.1 19.8 %collective-permute-start.43 = (f32[16,1,128]{2,1,0:T(1,128)S(1)}, f32[16,1,128]{2,1,0:T(1,128)S(1)}, u32[]{:S(2)}, u32[]{:S(2)}) collective-permute-start(f32[16,1,128]{2,1,0:T(1,128)S(1)} %get-tuple-element.88), channel_id=1, source_target_pairs={{0,1},{1,2},{2,3},{3,128},{128,129},{129,130},{130,131},{131,256},... | collective-permute-start | bytes 24584 | tf_op jit(solution)/shard_map/ppermute | solution.py:27
  596.5 21.7 %collective-permute-start.46 = (f32[16,1,128]{2,1,0:T(1,128)S(1)}, f32[16,1,128]{2,1,0:T(1,128)S(1)}, u32[]{:S(2)}, u32[]{:S(2)}) collective-permute-start(f32[16,1,128]{2,1,0:T(1,128)S(1)} %get-tuple-element.85), channel_id=1, source_target_pairs={{1,0},{2,1},{3,2},{128,3},{129,128},{130,129},{131,130},{256,131},... | collective-permute-start | bytes 24584 | tf_op jit(solution)/shard_map/ppermute | solution.py:28
  598.4 19.8 %collective-permute-start.47 = (f32[16,1,128]{2,1,0:T(1,128)S(1)}, f32[16,1,128]{2,1,0:T(1,128)S(1)}, u32[]{:S(2)}, u32[]{:S(2)}) collective-permute-start(f32[16,1,128]{2,1,0:T(1,128)S(1)} %get-tuple-element.84), channel_id=1, source_target_pairs={{0,1},{1,2},{2,3},{3,128},{128,129},{129,130},{130,131},{131,256},... | collective-permute-start | bytes 24584 | tf_op jit(solution)/shard_map/ppermute | solution.py:27
  622.9 21.7 %collective-permute-start.50 = (f32[16,1,128]{2,1,0:T(1,128)S(1)}, f32[16,1,128]{2,1,0:T(1,128)S(1)}, u32[]{:S(2)}, u32[]{:S(2)}) collective-permute-start(f32[16,1,128]{2,1,0:T(1,128)S(1)} %get-tuple-element.81), channel_id=1, source_target_pairs={{1,0},{2,1},{3,2},{128,3},{129,128},{130,129},{131,130},{256,131},... | collective-permute-start | bytes 24584 | tf_op jit(solution)/shard_map/ppermute | solution.py:28
  624.8 19.8 %collective-permute-start.51 = (f32[16,1,128]{2,1,0:T(1,128)S(1)}, f32[16,1,128]{2,1,0:T(1,128)S(1)}, u32[]{:S(2)}, u32[]{:S(2)}) collective-permute-start(f32[16,1,128]{2,1,0:T(1,128)S(1)} %get-tuple-element.80), channel_id=1, source_target_pairs={{0,1},{1,2},{2,3},{3,128},{128,129},{129,130},{130,131},{131,256},... | collective-permute-start | bytes 24584 | tf_op jit(solution)/shard_map/ppermute | solution.py:27
  649.2 41.5 %collective-permute-start.54 = (f32[16,1,128]{2,1,0:T(1,128)S(1)}, f32[16,1,128]{2,1,0:T(1,128)S(1)}, u32[]{:S(2)}, u32[]{:S(2)}) collective-permute-start(f32[16,1,128]{2,1,0:T(1,128)S(1)} %get-tuple-element.77), channel_id=1, source_target_pairs={{1,0},{2,1},{3,2},{128,3},{129,128},{130,129},{131,130},{256,131},... | collective-permute-start | bytes 24584 | tf_op jit(solution)/shard_map/ppermute | solution.py:28
  651.2 39.6 %collective-permute-start.55 = (f32[16,1,128]{2,1,0:T(1,128)S(1)}, f32[16,1,128]{2,1,0:T(1,128)S(1)}, u32[]{:S(2)}, u32[]{:S(2)}) collective-permute-start(f32[16,1,128]{2,1,0:T(1,128)S(1)} %get-tuple-element.76), channel_id=1, source_target_pairs={{0,1},{1,2},{2,3},{3,128},{128,129},{129,130},{130,131},{131,256},... | collective-permute-start | bytes 24584 | tf_op jit(solution)/shard_map/ppermute | solution.py:27
  665.6 25.1 %collective-permute-start.52 = (f32[1,8,128]{2,1,0:T(8,128)S(1)}, f32[1,8,128]{2,1,0:T(8,128)S(1)}, u32[]{:S(2)}, u32[]{:S(2)}) collective-permute-start(f32[1,8,128]{2,1,0:T(8,128)S(1)} %get-tuple-element.75), channel_id=1, source_target_pairs={{4,0},{8,4},{12,8},{16,12},{20,16},{24,20},{28,24},{32,28},{36,32}... | collective-permute-start | bytes 12296 | tf_op jit(solution)/shard_map/ppermute | solution.py:28
  667.6 23.2 %collective-permute-start.53 = (f32[1,8,128]{2,1,0:T(8,128)S(1)}, f32[1,8,128]{2,1,0:T(8,128)S(1)}, u32[]{:S(2)}, u32[]{:S(2)}) collective-permute-start(f32[1,8,128]{2,1,0:T(8,128)S(1)} %get-tuple-element.74), channel_id=1, source_target_pairs={{0,4},{4,8},{8,12},{12,16},{16,20},{20,24},{24,28},{28,32},{32,36}... | collective-permute-start | bytes 12296 | tf_op jit(solution)/shard_map/ppermute | solution.py:27
  686.4 156.6 %all-to-all-start.4 = ((f32[16,1,16384]{2,1,0:T(1,128)}), f32[16,1,16384]{2,1,0:T(1,128)S(1)}, u32[]{:S(2)}, u32[]{:S(2)}) async-start(f32[16,1,16384]{2,1,0:T(1,128)} %reshape.363), calls=%async_computation.4 | async-start | bytes 2097152 | tf_op jit(solution)/shard_map/all_to_all | solution.py:161
  691.1 23.6 %collective-permute-start.58 = (f32[16,1,128]{2,1,0:T(1,128)S(1)}, f32[16,1,128]{2,1,0:T(1,128)S(1)}, u32[]{:S(2)}, u32[]{:S(2)}) collective-permute-start(f32[16,1,128]{2,1,0:T(1,128)S(1)} %get-tuple-element.73), channel_id=1, source_target_pairs={{1,0},{2,1},{3,2},{128,3},{129,128},{130,129},{131,130},{256,131},... | collective-permute-start | bytes 24584 | tf_op jit(solution)/shard_map/ppermute | solution.py:28
  693.6 21.1 %collective-permute-start.59 = (f32[16,1,128]{2,1,0:T(1,128)S(1)}, f32[16,1,128]{2,1,0:T(1,128)S(1)}, u32[]{:S(2)}, u32[]{:S(2)}) collective-permute-start(f32[16,1,128]{2,1,0:T(1,128)S(1)} %get-tuple-element.72), channel_id=1, source_target_pairs={{0,1},{1,2},{2,3},{3,128},{128,129},{129,130},{130,131},{131,256},... | collective-permute-start | bytes 24584 | tf_op jit(solution)/shard_map/ppermute | solution.py:27
  729.3 21.7 %collective-permute-start.62 = (f32[8,1,64]{2,1,0:T(1,128)S(1)}, f32[8,1,64]{2,1,0:T(1,128)S(1)}, u32[]{:S(2)}, u32[]{:S(2)}) collective-permute-start(f32[8,1,64]{2,1,0:T(1,128)S(1)} %get-tuple-element.117), channel_id=1, source_target_pairs={{1,0},{2,1},{3,2},{128,3},{129,128},{130,129},{131,130},{256,131},... | collective-permute-start | bytes 6152 | tf_op jit(solution)/shard_map/ppermute | solution.py:28
  761.8 22.4 %collective-permute-start.66 = (f32[8,1,64]{2,1,0:T(1,128)S(1)}, f32[8,1,64]{2,1,0:T(1,128)S(1)}, u32[]{:S(2)}, u32[]{:S(2)}) collective-permute-start(f32[8,1,64]{2,1,0:T(1,128)S(1)} %get-tuple-element.113), channel_id=1, source_target_pairs={{1,0},{2,1},{3,2},{128,3},{129,128},{130,129},{131,130},{256,131},... | collective-permute-start | bytes 6152 | tf_op jit(solution)/shard_map/ppermute | solution.py:28
  763.7 20.5 %collective-permute-start.67 = (f32[8,1,64]{2,1,0:T(1,128)S(1)}, f32[8,1,64]{2,1,0:T(1,128)S(1)}, u32[]{:S(2)}, u32[]{:S(2)}) collective-permute-start(f32[8,1,64]{2,1,0:T(1,128)S(1)} %get-tuple-element.112), channel_id=1, source_target_pairs={{0,1},{1,2},{2,3},{3,128},{128,129},{129,130},{130,131},{131,256},... | collective-permute-start | bytes 6152 | tf_op jit(solution)/shard_map/ppermute | solution.py:27
  790.8 21.7 %collective-permute-start.70 = (f32[4,1,32]{2,0,1:T(4,128)S(1)}, f32[4,1,32]{2,0,1:T(4,128)S(1)}, u32[]{:S(2)}, u32[]{:S(2)}) collective-permute-start(f32[4,1,32]{2,0,1:T(4,128)S(1)} %get-tuple-element.145), channel_id=1, source_target_pairs={{1,0},{2,1},{3,2},{128,3},{129,128},{130,129},{131,130},{256,131},... | collective-permute-start | bytes 1544 | tf_op jit(solution)/shard_map/ppermute | solution.py:28
  817.0 21.7 %collective-permute-start.74 = (f32[4,1,32]{2,0,1:T(4,128)S(1)}, f32[4,1,32]{2,0,1:T(4,128)S(1)}, u32[]{:S(2)}, u32[]{:S(2)}) collective-permute-start(f32[4,1,32]{2,0,1:T(4,128)S(1)} %get-tuple-element.141), channel_id=1, source_target_pairs={{1,0},{2,1},{3,2},{128,3},{129,128},{130,129},{131,130},{256,131},... | collective-permute-start | bytes 1544 | tf_op jit(solution)/shard_map/ppermute | solution.py:28
  874.3 143.6 %all-to-all-start.5 = ((f32[32,1,8192]{2,1,0:T(1,128)}), f32[32,1,8192]{2,1,0:T(1,128)S(1)}, u32[]{:S(2)}, u32[]{:S(2)}) async-start(f32[32,1,8192]{2,1,0:T(1,128)} %reshape.365), calls=%async_computation.5 | async-start | bytes 2097152 | tf_op jit(solution)/shard_map/all_to_all | solution.py:167
  882.9 22.6 %collective-permute-start.78 = (f32[4,1,32]{2,0,1:T(4,128)S(1)}, f32[4,1,32]{2,0,1:T(4,128)S(1)}, u32[]{:S(2)}, u32[]{:S(2)}) collective-permute-start(f32[4,1,32]{2,0,1:T(4,128)S(1)} %get-tuple-element.137), channel_id=1, source_target_pairs={{1,0},{2,1},{3,2},{128,3},{129,128},{130,129},{131,130},{256,131},... | collective-permute-start | bytes 1544 | tf_op jit(solution)/shard_map/ppermute | solution.py:28
  884.8 20.8 %collective-permute-start.79 = (f32[4,1,32]{2,0,1:T(4,128)S(1)}, f32[4,1,32]{2,0,1:T(4,128)S(1)}, u32[]{:S(2)}, u32[]{:S(2)}) collective-permute-start(f32[4,1,32]{2,0,1:T(4,128)S(1)} %get-tuple-element.136), channel_id=1, source_target_pairs={{0,1},{1,2},{2,3},{3,128},{128,129},{129,130},{130,131},{131,256},... | collective-permute-start | bytes 1544 | tf_op jit(solution)/shard_map/ppermute | solution.py:27
  911.7 21.7 %collective-permute-start.82 = (f32[8,1,64]{2,1,0:T(1,128)S(1)}, f32[8,1,64]{2,1,0:T(1,128)S(1)}, u32[]{:S(2)}, u32[]{:S(2)}) collective-permute-start(f32[8,1,64]{2,1,0:T(1,128)S(1)} %get-tuple-element.109), channel_id=1, source_target_pairs={{1,0},{2,1},{3,2},{128,3},{129,128},{130,129},{131,130},{256,131},... | collective-permute-start | bytes 6152 | tf_op jit(solution)/shard_map/ppermute | solution.py:28
  937.9 21.7 %collective-permute-start.86 = (f32[8,1,64]{2,1,0:T(1,128)S(1)}, f32[8,1,64]{2,1,0:T(1,128)S(1)}, u32[]{:S(2)}, u32[]{:S(2)}) collective-permute-start(f32[8,1,64]{2,1,0:T(1,128)S(1)} %get-tuple-element.105), channel_id=1, source_target_pairs={{1,0},{2,1},{3,2},{128,3},{129,128},{130,129},{131,130},{256,131},... | collective-permute-start | bytes 6152 | tf_op jit(solution)/shard_map/ppermute | solution.py:28
  964.6 21.7 %collective-permute-start.90 = (f32[16,1,128]{2,1,0:T(1,128)S(1)}, f32[16,1,128]{2,1,0:T(1,128)S(1)}, u32[]{:S(2)}, u32[]{:S(2)}) collective-permute-start(f32[16,1,128]{2,1,0:T(1,128)S(1)} %get-tuple-element.69), channel_id=1, source_target_pairs={{1,0},{2,1},{3,2},{128,3},{129,128},{130,129},{131,130},{256,131},... | collective-permute-start | bytes 24584 | tf_op jit(solution)/shard_map/ppermute | solution.py:28
  966.5 19.8 %collective-permute-start.91 = (f32[16,1,128]{2,1,0:T(1,128)S(1)}, f32[16,1,128]{2,1,0:T(1,128)S(1)}, u32[]{:S(2)}, u32[]{:S(2)}) collective-permute-start(f32[16,1,128]{2,1,0:T(1,128)S(1)} %get-tuple-element.68), channel_id=1, source_target_pairs={{0,1},{1,2},{2,3},{3,128},{128,129},{129,130},{130,131},{131,256},... | collective-permute-start | bytes 24584 | tf_op jit(solution)/shard_map/ppermute | solution.py:27
  990.9 21.7 %collective-permute-start.94 = (f32[16,1,128]{2,1,0:T(1,128)S(1)}, f32[16,1,128]{2,1,0:T(1,128)S(1)}, u32[]{:S(2)}, u32[]{:S(2)}) collective-permute-start(f32[16,1,128]{2,1,0:T(1,128)S(1)} %get-tuple-element.65), channel_id=1, source_target_pairs={{1,0},{2,1},{3,2},{128,3},{129,128},{130,129},{131,130},{256,131},... | collective-permute-start | bytes 24584 | tf_op jit(solution)/shard_map/ppermute | solution.py:28
  992.9 19.8 %collective-permute-start.95 = (f32[16,1,128]{2,1,0:T(1,128)S(1)}, f32[16,1,128]{2,1,0:T(1,128)S(1)}, u32[]{:S(2)}, u32[]{:S(2)}) collective-permute-start(f32[16,1,128]{2,1,0:T(1,128)S(1)} %get-tuple-element.64), channel_id=1, source_target_pairs={{0,1},{1,2},{2,3},{3,128},{128,129},{129,130},{130,131},{131,256},... | collective-permute-start | bytes 24584 | tf_op jit(solution)/shard_map/ppermute | solution.py:27
  (60 other events, 620.7 us)
where the time goes:
time: 1060 us; the launch traced here: 1040 us
  starting transfers between devices  608 us (57%)
  waiting for transfers between devices  200 us (19%)
  local copies, waits for them, and re-layouts  120 us (11%)
  matrix products  60.9 us (6%)
  other arithmetic  32.9 us (3%)
  blocking collectives  18.9 us (2%)
    ppermute x48, starting transfers between devices, extended(): lax.ppermute(last, axis, up)  420 us
    ppermute x48, starting transfers between devices, extended(): lax.ppermute(initial, axis, [(b, a) for a, b in up])  111 us
    ppermute x48, waiting for transfers between devices, extended(): lax.ppermute(last, axis, up)  105 us
    all_to_all x1, waiting for transfers between devices, local(): lax.all_to_all(dense, ('group', 'gy'), split_axis=0, concat_axis=1, tiled...  50.5 us
    unnamed x26, local copies, waits for them, and re-layouts  37.6 us
    all_to_all x1, waiting for transfers between devices, local(): lax.all_to_all(dense, 'gx', split_axis=2, concat_axis=0, tiled=True)  37.1 us
    dot_general x4, matrix products, last_axis(): return jnp.einsum('abj,kj->abk', block, table, precision=HIGH)  26.1 us
  transfers between devices with their start and end apart: 103, of which 27 were waited for; matrix products, arithmetic and copies ran while one was open for 9% of the time, Pallas kernels for 0%

commit v1 on v0

v1 whole, which is shorter than its diff:
```python
import math

import jax
import jax.numpy as jnp
import numpy as np
from jax import lax
from jax.experimental import pallas as pl
from jax.experimental.pallas import tpu as pltpu
from jax.sharding import PartitionSpec as P

NP = 512
CYCLES = 2
LEVELS = 3
SWEEPS = 2
COARSE_SWEEPS = 4

OMEGA = 6.0 / 7.0
F32 = jnp.float32
BF16 = jnp.bfloat16
ALL = ("group", "gy", "gx")
GX = 32
YY = 16
WX = NP // GX
WY = NP // YY
SX = 256
SY = 64
SZ = 64
HX = 4
HY = 6
LANES = 128
FORE = 5
BACK = 6


def split(x):
    high = x.astype(BF16)
    return high, (x - high.astype(F32)).astype(BF16)


def product(a, b, dims):
    def dot(u, v):
        return lax.dot_general(u, v, (dims, ((), ())), preferred_element_type=F32)

    return dot(a[0], b[0]) + (dot(a[0], b[1]) + dot(a[1], b[0]))


NN = ((1,), (0,))
NT = ((1,), (1,))


def forward_kernel(offsets, mass, fine, high, low, pairs, out, beside):
    for i in range(8):
        beside[8 * i : 8 * i + 8, :] = fine[2 * i] + fine[2 * i + 1]
    both = beside[pl.ds(0, 32, stride=2), :] + beside[pl.ds(1, 32, stride=2), :]
    first = both.astype(BF16)
    left = both - first.astype(F32)
    second = left.astype(BF16)
    third = (left - second.astype(F32)).astype(BF16)
    add = pairs[...]

    def dot(u):
        return lax.dot_general(u, add, (NN, ((), ())), preferred_element_type=F32)

    rest = dot(first) + (dot(second) + dot(third))
    rest = jnp.concatenate([rest, jnp.zeros((96, LANES), F32)], axis=0)
    rest = jnp.concatenate([rest, jnp.zeros((LANES, NP - LANES), F32)], axis=1)
    rest = pltpu.roll(rest, offsets[2], 1)
    table = (high[...], low[...])
    dense = product(table, split(mass[...]), NT)
    for c in range(4):
        out[pl.ds(c, NP, stride=FORE), :] = dense[:, c * LANES : (c + 1) * LANES]
    out[pl.ds(4, NP, stride=FORE), :] = product(table, split(rest), NT)


def place(group, amount, shift, total, value):
    amount = amount % LANES
    if amount:
        value = pltpu.roll(value, amount, 1)
    if total is None:
        return value
    return jnp.where(group == shift, value, total)


def plane_kernel(offsets, wave, got, high, low, column, row, out, plane0, plane1, plane2, plane3, rest):
    plane = (plane0, plane1, plane2, plane3)
    lane = lax.broadcasted_iota(jnp.int32, (GX, LANES), 1)
    group = lane // WY
    for a in range(4):
        for b in range(4):
            parts = [got[pl.ds((b * 4 + q) * GX * FORE + a, GX, stride=FORE), :] for q in range(4)]
            for p in range(4):
                total = None
                for q in range(4):
                    total = place(group, (q - p) * WY, q, total, parts[q])
                plane[b][pl.ds(a * 4 + p, GX, stride=WX), :] = total
    light = lane // 4
    parts = [got[pl.ds(q * GX * FORE + 4, GX, stride=FORE), :] for q in range(YY)]
    for p in range(8):
        total = jnp.zeros((GX, LANES), F32)
        for q in range(YY):
            total = place(light, (q - p) * 4, q, total, parts[q])
        rest[pl.ds(p, GX, stride=8), :] = total
    wide = jnp.concatenate([rest[0:SX, :], jnp.zeros((SX, NP - LANES), F32)], axis=1)
    wide = pltpu.roll(wide, offsets[1], 1)
    wide = jnp.concatenate([wide, jnp.zeros((NP - SX, NP), F32)], axis=0)
    wide = pltpu.roll(wide, offsets[0], 0)
    table = (high[...], low[...])
    half = product(table, split(jnp.concatenate([part[...] for part in plane], axis=1) + wide), NN)
    spectrum = product(split(half), table, NN)
    lam = column[...] + (row[...] + wave[0])
    spectrum = spectrum * jnp.where(lam > 0, (1.0 / float(NP**3)) / jnp.where(lam > 0, lam, 1.0), 0.0)
    half = product(split(spectrum), table, NN)
    whole = product(table, split(half), NN)
    for b in range(4):
        plane[b][...] = whole[:, b * LANES : (b + 1) * LANES]
    near = pltpu.roll(whole, (NP - offsets[0]) % NP, 0)[0:SX, :]
    near = pltpu.roll(near, (NP + HY - offsets[1]) % NP, 1)[:, 0:LANES]
    place_of = lax.broadcasted_iota(jnp.int32, (SX, LANES), 1)
    near = jnp.where(place_of < HY, near[:, HY : HY + 1], near)
    near = jnp.where(place_of >= HY + SY, near[:, HY + SY - 1 : HY + SY], near)
    rest[HX : HX + SX, :] = near
    rest[0:HX, :] = jnp.broadcast_to(near[0:1, :], (HX, LANES))
    rest[HX + SX : 2 * HX + SX, :] = jnp.broadcast_to(near[SX - 1 : SX, :], (HX, LANES))
    for a in range(4):
        for b in range(4):
            parts = [plane[b][pl.ds(a * 4 + p, GX, stride=WX), :] for p in range(4)]
            for q in range(4):
                total = None
                for p in range(4):
                    total = place(group, (p - q) * WY, p, total, parts[p])
                out[pl.ds((b * 4 + q) * GX * BACK + a, GX, stride=BACK), :] = total
    wing = lane // 16
    for h in range(2):
        parts = [rest[pl.ds(h * 8 + p, GX, stride=8), :] for p in range(8)]
        for q in range(YY):
            total = None
            for p in range(8):
                total = place(wing, p * 16 - 4 * q, p, total, parts[p])
            out[pl.ds(q * GX * BACK + 4 + h, GX, stride=BACK), :] = total


def near_kernel(offsets, got, high, low, out):
    table = (high[...], low[...])
    back = (NP - offsets[2]) % NP
    for h in range(2):
        turned = got[pl.ds(4 + h, NP, stride=BACK), :].T
        rows = product(split(turned), table, NN)
        out[h * LANES : (h + 1) * LANES, :] = pltpu.roll(rows, back, 1)[:, 0:LANES]


def whole_kernel(got, high, low, out):
    table = (high[...], low[...])
    for c in range(4):
        turned = got[pl.ds(c, NP, stride=BACK), :].T
        out[c * LANES : (c + 1) * LANES, :] = product(split(turned), table, NN)


def cas_tables():
    wave = np.arange(NP)
    angle = (wave[:, None] * wave[None, :] % NP) * (2.0 * np.pi / NP)
    return jnp.asarray((np.cos(angle) + np.sin(angle)).astype(np.float32))


def eigenvalues():
    sine = np.sin(np.arange(NP) * (np.pi / NP))
    return (4.0 * sine * sine).astype(np.float32)


VMEM = pl.BlockSpec(memory_space=pltpu.VMEM)
SMEM = pl.BlockSpec(memory_space=pltpu.SMEM)
PARAMS = pltpu.CompilerParams(vmem_limit_bytes=56 * 1024 * 1024)
INTERPRET = False


def call(body, name, ins, shape, scratch=()):
    return pl.pallas_call(
        body,
        name=name,
        in_specs=ins,
        out_specs=VMEM,
        out_shape=jax.ShapeDtypeStruct(shape, F32),
        scratch_shapes=list(scratch),
        compiler_params=PARAMS,
        interpret=INTERPRET,
    )


def forward(offsets, mass, fine, high, low, pairs):
    return call(forward_kernel, "forward", [SMEM] + [VMEM] * 5, (NP * FORE, LANES), [pltpu.VMEM((64, LANES), F32)])(
        offsets, mass, fine, high, low, pairs
    )


def spectral(offsets, wave, got, high, low, column, row):
    return call(
        plane_kernel,
        "plane",
        [SMEM, SMEM] + [VMEM] * 5,
        (NP * BACK, LANES),
        [pltpu.VMEM((NP, LANES), F32)] * 4 + [pltpu.VMEM((SX + 8, LANES), F32)],
    )(offsets, wave, got, high, low, column, row)


def near_back(offsets, got, high, low):
    return call(near_kernel, "near", [SMEM] + [VMEM] * 3, (256, LANES))(offsets, got, high, low)


def whole_back(got, high, low):
    return call(whole_kernel, "whole", [VMEM] * 3, (NP, NP))(got, high, low)


def swap(piece, lanes):
    piece = piece.reshape(NP, 1, lanes)
    return lax.all_to_all(piece, ALL, 0, 0, tiled=True).reshape(NP * lanes // LANES, LANES)


def constants():
    high, low = split(cas_tables())
    pairs = np.zeros((LANES, LANES), np.float32)
    pairs[np.arange(LANES), np.arange(LANES) // 2] = 1.0
    eigen = eigenvalues()
    return high, low, jnp.asarray(pairs, BF16), jnp.asarray(eigen[:, None]), jnp.asarray(eigen[None, :]), jnp.asarray(eigen)


XF = 32
YF = 24
X1 = 40
Y1 = 64
X2 = 20
Y2 = 32
STEP = 1.0 / 7.0


def exact(value, table):
    first = value.astype(BF16)
    left = value - first.astype(F32)
    second = left.astype(BF16)
    third = (left - second.astype(F32)).astype(BF16)

    def dot(u):
        return lax.dot_general(u, table, (NN, ((), ())), preferred_element_type=F32)

    return dot(first) + (dot(second) + dot(third))


def over(count, body, per=4):
    def group(t, carry):
        for k in range(per):
            body(t * per + k)
        return carry

    lax.fori_loop(0, count // per, group, 0)


def lanes_of(rows):
    return lax.broadcasted_iota(jnp.int32, (rows, LANES), 1)


def rows_of(rows):
    return lax.broadcasted_iota(jnp.int32, (rows, LANES), 0)


def inside(place, count):
    return jnp.where((place >= 0) & (place < count), 1.0, 0.0).astype(F32)


class Fine:
    def __init__(self, pos):
        self.first = 16 * pos[0] - 8
        self.count = 512
        self.x = XF
        y = rows_of(YF) + (8 * pos[1] - 8)
        self.mask = jnp.where((y >= 0) & (y < 128), STEP, 0.0)
        lane = lanes_of(YF)
        self.low = jnp.where(lane == 0, 0.0, 1.0)
        self.high = jnp.where(lane == LANES - 1, 0.0, 1.0)

    def around(self, ref, x):
        c = ref[x + 1]
        near = ref[x] + ref[x + 2]
        near = near + (pltpu.roll(c, 1, 0) + pltpu.roll(c, YF - 1, 0))
        near = near + (pltpu.roll(c, 1, 1) * self.low + pltpu.roll(c, LANES - 1, 1) * self.high)
        return c, near


class Coarse:
    def __init__(self, first, count, x, y, z):
        self.first = first
        self.count = count
        self.x = x
        self.y = y
        self.mask = jnp.where(lanes_of(y) < z, STEP, 0.0)
        row = rows_of(y)
        self.low = jnp.where(row == 0, 0.0, 1.0)
        self.high = jnp.where(row == y - 1, 0.0, 1.0)

    def around(self, ref, x):
        c = ref[x + 1]
        near = ref[x] + ref[x + 2]
        near = near + (pltpu.roll(c, 1, 0) * self.low + pltpu.roll(c, self.y - 1, 0) * self.high)
        near = near + (pltpu.roll(c, 1, 1) + pltpu.roll(c, LANES - 1, 1))
        return c, near


def sweep(level, source, right, shift, target):
    def body(x):
        c, near = level.around(source, x)
        scale = inside(level.first + x, level.count)
        target[x + 1] = (right[x + shift] + (c + near)) * (level.mask * scale)

    over(level.x, body)


def clear(ref, size):
    ref[0] = jnp.zeros(ref.shape[1:], F32)
    ref[size + 1] = jnp.zeros(ref.shape[1:], F32)


def lower_of(level, corr, resid, strip, pairs, out):
    def left(x):
        c, near = level.around(corr, x)
        return (resid[x] - (6.0 * c - near))[8:16]

    for k in range(8):
        strip[8 * k : 8 * k + 8, :] = left(8 + 2 * k) + left(9 + 2 * k)
    both = strip[pl.ds(0, 32, stride=2), :] + strip[pl.ds(1, 32, stride=2), :]
    small = 0.5 * exact(both, pairs)
    out[...] = small[0:16] + pltpu.roll(small[16:32], 64, 1)


def open_kernel(pos, near, fine, pairs, spread, start, resid, corr, lower, wide, first, second, tall, twice, strip):
    level = Fine(pos)
    tall[...] = exact(near[...], spread[...])
    for i in range(16):
        value = tall[i * 16 + 2 : i * 16 + 14, :]
        twice[pl.ds(0, 12, stride=2), :] = value
        twice[pl.ds(1, 12, stride=2), :] = value
        wide[1 + 2 * i] = twice[...]
        wide[2 + 2 * i] = twice[...]
    clear(wide, XF)
    clear(first, XF)
    clear(second, XF)
    for k in range(16):
        start[k] = wide[9 + k][8:16]

    def body(x):
        c, around = level.around(wide, x)
        edge = c * ((1.0 - level.low) + (1.0 - level.high))
        value = 2.0 * fine[x] - (6.0 * c - (around + edge))
        scale = inside(level.first + x, level.count)
        held = jnp.where(level.mask * scale > 0.0, value, 0.0)
        resid[x] = held
        first[x + 1] = held * STEP

    over(XF, body)
    sweep(level, first, resid, 0, second)
    corr[...] = second[1 : XF + 1]
    lower_of(level, second, resid, strip, pairs[...], lower)


def coarse(pos, blocks, corr, resid, pairs, spread, one, scratch):
    right1, left1, other1, right2, left2, other2, rows, double, grown, twice, first, second = scratch
    level1 = Coarse(8 * pos[0] - 16, 256, X1, Y1, 64)
    level2 = Coarse(4 * pos[0] - 8, 128, X2, Y2, 32)
    fine = Fine(pos)
    lane = lanes_of(Y1)
    for ref in (left1, other1):
        clear(ref, X1)
    for ref in (left2, other2):
        clear(ref, X2)
    for b, block in enumerate(blocks):
        for xx in range(4):
            value = block[xx]
            for half in range(2):
                held = jnp.where(lane < 64, pltpu.roll(value, 64, 1) if half else value, 0.0)
                right1[b * 8 + half * 4 + xx] = held
                left1[1 + b * 8 + half * 4 + xx] = held * STEP
    sweep(level1, left1, right1, 0, other1)

    def down(k):
        total = None
        for a in range(2):
            c, near = level1.around(other1, 2 * k + a)
            value = right1[2 * k + a] - (6.0 * c - near)
            total = value if total is None else total + value
        double[...] = total
        rows[pl.ds(pl.multiple_of(k * Y2, Y2), Y2), :] = double[pl.ds(0, Y2, stride=2), :] + double[pl.ds(1, Y2, stride=2), :]

    over(X2, down, 1)
    rows[...] = exact(rows[...], pairs)

    def begin(k):
        value = rows[pl.ds(pl.multiple_of(k * Y2, Y2), Y2), :]
        scale = inside(level2.first + k, level2.count)
        value = jnp.where(level2.mask * scale > 0.0, 0.5 * value, 0.0)
        right2[k] = value
        left2[k + 1] = value * STEP

    over(X2, begin)
    sweep(level2, left2, right2, 0, other2)
    sweep(level2, other2, right2, 0, left2)
    sweep(level2, left2, right2, 0, other2)
    rows[...] = exact(other2[1 : X2 + 1].reshape(X2 * Y2, LANES), spread)

    def up(k):
        value = rows[pl.ds(pl.multiple_of(k * Y2, Y2), Y2), :]
        double[pl.ds(0, Y2, stride=2), :] = value
        double[pl.ds(1, Y2, stride=2), :] = value
        value = double[...]
        other1[1 + 2 * k] = other1[1 + 2 * k] + value
        other1[2 + 2 * k] = other1[2 + 2 * k] + value

    over(X2, up, 1)
    sweep(level1, other1, right1, 0, left1)
    sweep(level1, left1, right1, 0, other1)
    amount = 124 - 4 * pos[1]
    for k in range(16):
        value = other1[13 + k]
        value = jnp.concatenate([jnp.zeros((8, LANES), F32), value, jnp.zeros((56, LANES), F32)], axis=0)
        grown[k * 16 : k * 16 + 16, :] = pltpu.roll(value, amount, 0)[0:16]
    grown[...] = exact(grown[...], spread)
    clear(first, XF)
    clear(second, XF)
    for i in range(16):
        value = grown[i * 16 : i * 16 + 12, :]
        twice[pl.ds(0, 12, stride=2), :] = value
        twice[pl.ds(1, 12, stride=2), :] = value
        first[1 + 2 * i] = corr[2 * i] + twice[...]
        first[2 + 2 * i] = corr[2 * i + 1] + twice[...]
    sweep(fine, first, resid, 0, second)
    sweep(fine, second, resid, 0, first)
    return fine


def turn_kernel(pos, b0, b1, b2, b3, b4, corr, resid, pairs, spread, after, lower, *scratch):
    strip, scratch = scratch[-1], scratch[:-1]
    fine = coarse(pos, (b0, b1, b2, b3, b4), corr, resid, pairs[...], spread[...], None, scratch)
    first, second = scratch[-2:]
    sweep(fine, first, resid, 0, second)
    sweep(fine, second, resid, 0, first)
    after[...] = first[1 : XF + 1]
    lower_of(fine, first, resid, strip, pairs[...], lower)


def close_kernel(pos, b0, b1, b2, b3, b4, corr, resid, pairs, spread, start, out, *scratch):
    coarse(pos, (b0, b1, b2, b3, b4), corr, resid, pairs[...], spread[...], None, scratch)
    first = scratch[-2]
    for k in range(16):
        out[k] = start[k] + first[9 + k][8:16]


def held(*shape):
    return pltpu.VMEM(shape, F32)


def shaped(*shape):
    return jax.ShapeDtypeStruct(shape, F32)


def inner():
    return [
        held(X1, Y1, LANES),
        held(X1 + 2, Y1, LANES),
        held(X1 + 2, Y1, LANES),
        held(X2, Y2, LANES),
        held(X2 + 2, Y2, LANES),
        held(X2 + 2, Y2, LANES),
        held(X2 * Y2, LANES),
        held(Y1, LANES),
        held(256, LANES),
        held(YF, LANES),
        held(XF + 2, YF, LANES),
        held(XF + 2, YF, LANES),
    ]


def many(body, name, count, shapes, scratch):
    return pl.pallas_call(
        body,
        name=name,
        in_specs=[SMEM] + [VMEM] * count,
        out_specs=[VMEM] * len(shapes),
        out_shape=shapes,
        scratch_shapes=scratch,
        compiler_params=PARAMS,
        interpret=INTERPRET,
    )


def opening(pos, near, fine, pairs, spread):
    shapes = [shaped(16, 8, LANES), shaped(XF, YF, LANES), shaped(XF, YF, LANES), shaped(16, LANES)]
    scratch = [held(XF + 2, YF, LANES)] * 3 + [held(256, LANES), held(YF, LANES), held(64, LANES)]
    return many(open_kernel, "opening", 4, shapes, scratch)(pos, near, fine, pairs, spread)


def turning(pos, blocks, corr, resid, pairs, spread):
    shapes = [shaped(XF, YF, LANES), shaped(16, LANES)]
    return many(turn_kernel, "turning", 9, shapes, inner() + [held(64, LANES)])(pos, *blocks, corr, resid, pairs, spread)


def closing(pos, blocks, corr, resid, pairs, spread, start):
    return many(close_kernel, "closing", 10, [shaped(16, 8, LANES)], inner())(
        pos, *blocks, corr, resid, pairs, spread, start
    )[0]


def shifted(value, axes, size, step):
    return lax.ppermute(value, axes, [(i, i + step) for i in range(size) if 0 <= i + step < size])


def gather(lower):
    every = jnp.broadcast_to(lower[None], (YY, 16, LANES))
    every = lax.all_to_all(every, ("group", "gy"), 0, 0, tiled=True)
    block = every.reshape(YY, 4, 4, LANES).transpose(1, 0, 2, 3).reshape(4, Y1, LANES)
    return [block if step == 0 else shifted(block, "gx", GX, step) for step in (2, 1, 0, -1, -2)]


def widened(fine):
    sides = ("group", "gy")
    tall = jnp.concatenate([shifted(fine, sides, YY, 1), fine, shifted(fine, sides, YY, -1)], axis=1)
    before = shifted(tall[8:16], "gx", GX, 1)
    behind = shifted(tall[0:8], "gx", GX, -1)
    return jnp.concatenate([before, tall, behind], axis=0)


def local(parent_mass, fine_mass, offsets):
    high, low, pairs, column, row, eigen = constants()
    spread = pairs.T
    pos = jnp.stack([lax.axis_index("gx"), lax.axis_index(("group", "gy"))]).astype(jnp.int32)
    wave = lax.dynamic_slice(eigen, (lax.axis_index(ALL),), (1,))
    wide = widened(fine_mass)
    got = swap(forward(offsets, parent_mass.reshape(NP, NP), fine_mass, high, low, pairs), FORE * LANES)
    got = swap(spectral(offsets, wave, got, high, low, column, row), BACK * LANES)
    near = near_back(offsets, got, high, low)
    start, resid, corr, lower = opening(pos, near, wide, pairs, spread)
    potential = whole_back(got, high, low)
    corr, lower = turning(pos, gather(lower), corr, resid, pairs, spread)
    out = closing(pos, gather(lower), corr, resid, pairs, spread, start)
    return (potential.reshape(WX, WY, NP), out)


def solution(mesh):
    spec = P("gx", ("group", "gy"), None)
    return jax.shard_map(
        local,
        mesh=mesh,
        in_specs=(spec, spec, P()),
        out_specs=(spec, spec),
        check_vma=False,
    )
```

time: 1060 us -> 328 us (0.31)
  the two profiles are of different devices: /device:TPU:135 before, /device:TPU:120 now
where the time goes in v1:
time: 328 us; the launch traced here: 327 us
  waiting for transfers between devices  136 us (41%)
  starting transfers between devices  78.7 us (24%)
  Pallas kernels  54.5 us (17%)
  blocking collectives  49.8 us (15%)
  local copies, waits for them, and re-layouts  6.46 us (2%)
    all_to_all x2, waiting for transfers between devices, swap(): lax.all_to_all(piece, ALL, 0, 0, tiled=True)  69 us
    ppermute x12, waiting for transfers between devices, shifted(): lax.ppermute(value, axes, [(i, i + step) for i in range(size) if 0 <= i +...  66.6 us
    all_to_all x2, blocking collectives, gather(): every = lax.all_to_all(every, ('group', 'gy'), 0, 0, tiled=True)  49.8 us
    ppermute x12, starting transfers between devices, shifted(): lax.ppermute(value, axes, [(i, i + step) for i in range(size) if 0 <= i +...  43.2 us
    all_to_all x2, starting transfers between devices, swap(): lax.all_to_all(piece, ALL, 0, 0, tiled=True)  35.5 us
    pallas_call x1, Pallas kernels, turning(): many(turn_kernel, 'turning', 9, shapes, inner() + [held(64, LANES)])  15.4 us
    pallas_call x1, Pallas kernels, closing(): many(close_kernel, 'closing', 10, [shaped(16, 8, LANES)], inner())  13.4 us
    pallas_call x1, Pallas kernels, spectral(): call(plane_kernel, 'plane', [SMEM, SMEM] + [VMEM] * 5, (NP * BACK, LANES)...  11 us
  transfers between devices with their start and end apart: 14, of which 9 were waited for; matrix products, arithmetic and copies ran while one was open for 1% of the time, Pallas kernels for 1%

profile of v1, /device:TPU:120, one launch (start us, length us, event | category | flops | bytes accessed | tf_op | source)
XLA Modules:
  0.0 327.5 jit_solution(7377180237678400049)
XLA Ops:
  0.6 4.1 %forward.1 = f32[2560,128]{1,0:T(8,128)} custom-call(s32[3]{0:T(128)} %offsets.5, f32[512,512]{1,0:T(8,128)} %bitcast.22, f32[16,8,128]{2,1,0:T(8,128)} %fine.1, bf16[512,512]{1,0:T(8,128)(2,1)} %constant.40.high, bf16[512,512]{1,0:T(8,128)(2,1)} %constant.43.low, bf16[128,128]{1,0:T(8,128)(2,1)} %constant.34.clone.pairs), custom_call_target="tpu_custom_call" | custom-call | tf_op jit(solution)/shard_map/forward/pallas_call | solution.py:189
  4.7 22.5 %all-to-all-start = ((f32[512,1,640]{2,1,0:T(1,128)}), f32[512,1,640]{2,1,0:T(1,128)S(1)}, u32[]{:S(2)}, u32[]{:S(2)}) async-start(f32[512,1,640]{2,1,0:T(1,128)} %bitcast.20), calls=%async_computation | async-start | bytes 2621440 | tf_op jit(solution)/shard_map/all_to_all | solution.py:214
  27.3 1.3 dynamic_slice.3.wave
  28.5 62.8 %all-to-all-done = f32[512,1,640]{2,1,0:T(1,128)S(1)} async-done(((f32[512,1,640]{2,1,0:T(1,128)}), f32[512,1,640]{2,1,0:T(1,128)S(1)}, u32[]{:S(2)}, u32[]{:S(2)}) %all-to-all-start) | async-done | bytes 1310752 | tf_op jit(solution)/shard_map/all_to_all | solution.py:214
  91.3 1.1 copy-done.1
  92.4 11.0 %plane.1 = f32[3072,128]{1,0:T(8,128)} custom-call(s32[3]{0:T(128)} %offsets.5, f32[1]{0:T(128)} %dynamic_slice.3.wave, f32[2560,128]{1,0:T(8,128)} %bitcast.19, bf16[512,512]{1,0:T(8,128)(2,1)} %constant.40.high, bf16[512,512]{1,0:T(8,128)(2,1)} %constant.43.low, f32[512,1]{1,0:T(8,128)} %constant.35.clone.column, f32[1,512]{1,0:T(1,128)} %constant.36.clone.row), custom_call_target="tpu_custom_call" | custom-call | tf_op jit(solution)/shard_map/plane/pallas_call | solution.py:195
  103.3 13.0 %all-to-all-start.1 = ((f32[512,1,768]{2,1,0:T(1,128)}), f32[512,1,768]{2,1,0:T(1,128)S(1)}, u32[]{:S(2)}, u32[]{:S(2)}) async-start(f32[512,1,768]{2,1,0:T(1,128)} %bitcast.18), calls=%async_computation.1 | async-start | bytes 3145728 | tf_op jit(solution)/shard_map/all_to_all | solution.py:214
  116.3 3.4 %collective-permute-start = (f32[16,8,128]{2,1,0:T(8,128)S(1)}, f32[16,8,128]{2,1,0:T(8,128)S(1)}, u32[]{:S(2)}, u32[]{:S(2)}) collective-permute-start(f32[16,8,128]{2,1,0:T(8,128)S(1)} %copy-done.4), channel_id=1, source_target_pairs={{0,1},{1,2},{2,3},{3,128},{128,129},{129,130},{130,131},{131,256},... | collective-permute-start | bytes 196616 | tf_op jit(solution)/shard_map/ppermute | solution.py:508
  119.7 1.3 collective-permute-start.1
  121.0 0.7 collective-permute-done
  121.7 4.4 %collective-permute-done.1 = f32[16,8,128]{2,1,0:T(8,128)S(1)} collective-permute-done((f32[16,8,128]{2,1,0:T(8,128)S(1)}, f32[16,8,128]{2,1,0:T(8,128)S(1)}, u32[]{:S(2)}, u32[]{:S(2)}) %collective-permute-start.1) | collective-permute-done | bytes 65568 | tf_op jit(solution)/shard_map/ppermute | solution.py:508
  126.1 3.0 collective-permute-start.3
  129.0 6.4 %collective-permute-start.2 = (f32[8,24,128]{2,1,0:T(8,128)S(1)}, f32[8,24,128]{2,1,0:T(8,128)S(1)}, u32[]{:S(2)}, u32[]{:S(2)}) collective-permute-start(f32[8,24,128]{2,1,0:T(8,128)S(1)} %get-tuple-element.14), channel_id=1, source_target_pairs={{0,4},{4,8},{8,12},{12,16},{16,20},{20,24},{24,28},{28,32},{32,36}... | collective-permute-start | bytes 294920 | tf_op jit(solution)/shard_map/ppermute | solution.py:508
  135.4 0.6 pad_add_fusion.pos
  136.0 48.7 %collective-permute-done.3 = f32[8,24,128]{2,1,0:T(8,128)S(1)} collective-permute-done((f32[8,24,128]{2,1,0:T(8,128)S(1)}, f32[8,24,128]{2,1,0:T(8,128)S(1)}, u32[]{:S(2)}, u32[]{:S(2)}) %collective-permute-start.3) | collective-permute-done | bytes 98336 | tf_op jit(solution)/shard_map/ppermute | solution.py:508
  184.7 0.0 collective-permute-done.2
  184.7 0.8 pad_maximum_fusion.fine
  185.5 6.3 %all-to-all-done.1 = f32[512,1,768]{2,1,0:T(1,128)S(1)} async-done(((f32[512,1,768]{2,1,0:T(1,128)}), f32[512,1,768]{2,1,0:T(1,128)S(1)}, u32[]{:S(2)}, u32[]{:S(2)}) %all-to-all-start.1) | async-done | bytes 1572896 | tf_op jit(solution)/shard_map/all_to_all | solution.py:214
  191.8 1.2 copy-done
  193.0 3.1 near.1
  196.0 4.0 %opening.1 = (f32[16,8,128]{2,1,0:T(8,128)}, f32[32,24,128]{2,1,0:T(8,128)}, f32[32,24,128]{2,1,0:T(8,128)}, f32[16,128]{1,0:T(8,128)}) custom-call(s32[2]{0:T(128)} %pad_add_fusion.pos, f32[256,128]{1,0:T(8,128)} %near.1, f32[32,24,128]{2,1,0:T(8,128)} %pad_maximum_fusion.fine, bf16[128,128]{1,0:T(8,128)(2,1)} %constant.34.clone.pairs, ...), custom_call_target="tpu_custom_call" | custom-call | tf_op jit(solution)/shard_map/opening/pallas_call | solution.py:493
  200.0 0.7 broadcast_in_dim.4
  200.7 31.7 %all_to_all.20 = f32[16,16,128]{2,1,0:T(8,128)S(1)} all-to-all(f32[16,16,128]{2,1,0:T(8,128)S(1)} %broadcast_in_dim.4), channel_id=1, replica_groups=mesh['group'=4,'gx'=32,'gy'=4] {'group','gy'}, dimensions={0} | all-to-all | bytes 262144 | tf_op jit(solution)/shard_map/all_to_all | solution.py:513
  232.5 0.1 copy.15
  232.5 3.4 %collective-permute-start.4 = (f32[4,64,128]{2,1,0:T(8,128)S(1)}, f32[4,64,128]{2,1,0:T(8,128)S(1)}, u32[]{:S(2)}, u32[]{:S(2)}) collective-permute-start(f32[4,64,128]{2,1,0:T(8,128)S(1)} %bitcast.30), channel_id=1, source_target_pairs={{0,8},{4,12},{8,16},{12,20},{16,24},{20,28},{24,32},{28,36},{32,40... | collective-permute-start | bytes 393224 | tf_op jit(solution)/shard_map/ppermute | solution.py:508
  235.9 5.7 %collective-permute-start.5 = (f32[4,64,128]{2,1,0:T(8,128)S(1)}, f32[4,64,128]{2,1,0:T(8,128)S(1)}, u32[]{:S(2)}, u32[]{:S(2)}) collective-permute-start(f32[4,64,128]{2,1,0:T(8,128)S(1)} %bitcast.31), channel_id=1, source_target_pairs={{0,4},{4,8},{8,12},{12,16},{16,20},{20,24},{24,28},{28,32},{32,36}... | collective-permute-start | bytes 393224 | tf_op jit(solution)/shard_map/ppermute | solution.py:508
  241.6 1.9 collective-permute-start.6
  243.6 3.7 %collective-permute-start.7 = (f32[4,64,128]{2,1,0:T(8,128)S(1)}, f32[4,64,128]{2,1,0:T(8,128)S(1)}, u32[]{:S(2)}, u32[]{:S(2)}) collective-permute-start(f32[4,64,128]{2,1,0:T(8,128)S(1)} %bitcast.33), channel_id=1, source_target_pairs={{8,0},{12,4},{16,8},{20,12},{24,16},{28,20},{32,24},{36,28},{40,32... | collective-permute-start | bytes 393224 | tf_op jit(solution)/shard_map/ppermute | solution.py:508
  247.2 0.0 collective-permute-done.4.b0
  247.2 0.0 copy-start.9
  247.2 0.0 collective-permute-done.5.b1
  247.3 5.6 %collective-permute-done.6.b3 = f32[4,64,128]{2,1,0:T(8,128)S(1)} collective-permute-done((f32[4,64,128]{2,1,0:T(8,128)S(1)}, f32[4,64,128]{2,1,0:T(8,128)S(1)}, u32[]{:S(2)}, u32[]{:S(2)}) %collective-permute-start.6) | collective-permute-done | bytes 131104 | tf_op jit(solution)/shard_map/ppermute | solution.py:508
  252.9 1.8 collective-permute-done.7.b4
  254.6 0.6 copy-done.12
  255.3 15.4 %turning.1 = (f32[32,24,128]{2,1,0:T(8,128)}, f32[16,128]{1,0:T(8,128)}) custom-call(s32[2]{0:T(128)} %pad_add_fusion.pos, f32[4,64,128]{2,1,0:T(8,128)} %copy-done.9, f32[4,64,128]{2,1,0:T(8,128)} %copy-done.10, f32[4,64,128]{2,1,0:T(8,128)} %bitcast.34, f32[4,64,128]{2,1,0:T(8,128)} %copy-done.11, f32[4,64,128]{2,1,0:T(8,128)} %copy-done.12, ...), custom_call_target="tpu_custom_call" | custom-call | tf_op jit(solution)/shard_map/turning/pallas_call | solution.py:498
  270.6 0.7 broadcast_in_dim.5
  271.3 18.1 %all_to_all.21 = f32[16,16,128]{2,1,0:T(8,128)S(1)} all-to-all(f32[16,16,128]{2,1,0:T(8,128)S(1)} %broadcast_in_dim.5), channel_id=1, replica_groups=mesh['group'=4,'gx'=32,'gy'=4] {'group','gy'}, dimensions={0} | all-to-all | bytes 262144 | tf_op jit(solution)/shard_map/all_to_all | solution.py:513
  289.5 0.1 copy.17
  289.5 5.3 %collective-permute-start.8 = (f32[4,64,128]{2,1,0:T(8,128)S(1)}, f32[4,64,128]{2,1,0:T(8,128)S(1)}, u32[]{:S(2)}, u32[]{:S(2)}) collective-permute-start(f32[4,64,128]{2,1,0:T(8,128)S(1)} %bitcast.23), channel_id=1, source_target_pairs={{0,8},{4,12},{8,16},{12,20},{16,24},{20,28},{24,32},{28,36},{32,40... | collective-permute-start | bytes 393224 | tf_op jit(solution)/shard_map/ppermute | solution.py:508
  294.8 5.4 %collective-permute-start.9 = (f32[4,64,128]{2,1,0:T(8,128)S(1)}, f32[4,64,128]{2,1,0:T(8,128)S(1)}, u32[]{:S(2)}, u32[]{:S(2)}) collective-permute-start(f32[4,64,128]{2,1,0:T(8,128)S(1)} %bitcast.24), channel_id=1, source_target_pairs={{0,4},{4,8},{8,12},{12,16},{16,20},{20,24},{24,28},{28,32},{32,36}... | collective-permute-start | bytes 393224 | tf_op jit(solution)/shard_map/ppermute | solution.py:508
  300.3 1.9 collective-permute-start.10
  302.2 1.9 collective-permute-start.11
  304.1 3.7 %whole.1 = f32[512,512]{1,0:T(8,128)} custom-call(f32[3072,128]{1,0:T(8,128)} %bitcast.17, bf16[512,512]{1,0:T(8,128)(2,1)} %constant.40.high, bf16[512,512]{1,0:T(8,128)(2,1)} %constant.43.low), custom_call_target="tpu_custom_call" | custom-call | tf_op jit(solution)/shard_map/whole/pallas_call | solution.py:209
  307.8 0.0 collective-permute-done.9.b1
  307.8 4.6 %collective-permute-done.10.b3 = f32[4,64,128]{2,1,0:T(8,128)S(1)} collective-permute-done((f32[4,64,128]{2,1,0:T(8,128)S(1)}, f32[4,64,128]{2,1,0:T(8,128)S(1)}, u32[]{:S(2)}, u32[]{:S(2)}) %collective-permute-start.10) | collective-permute-done | bytes 131104 | tf_op jit(solution)/shard_map/ppermute | solution.py:508
  312.4 1.0 collective-permute-done.11.b4
  313.4 0.6 copy-done.8
  314.1 13.4 %closing.1 = f32[16,8,128]{2,1,0:T(8,128)} custom-call(s32[2]{0:T(128)} %pad_add_fusion.pos, f32[4,64,128]{2,1,0:T(8,128)} %copy-done.5, f32[4,64,128]{2,1,0:T(8,128)} %copy-done.6, f32[4,64,128]{2,1,0:T(8,128)} %bitcast.27, f32[4,64,128]{2,1,0:T(8,128)} %copy-done.7, f32[4,64,128]{2,1,0:T(8,128)} %copy-done.8, f32[32,24,128]{2,1,0:T(8,128)} %get-tuple-element.12.corr, ...), custom_call_target="tpu_custom_call" | custom-call | tf_op jit(solution)/shard_map/closing/pallas_call | solution.py:502
  (28 shorter events, 0.2 us)
Async XLA Ops:
  4.7 86.6 %all-to-all-start = ((f32[512,1,640]{2,1,0:T(1,128)}), f32[512,1,640]{2,1,0:T(1,128)S(1)}, u32[]{:S(2)}, u32[]{:S(2)}) async-start(f32[512,1,640]{2,1,0:T(1,128)} %bitcast.20), calls=%async_computation | async-start | bytes 2621440 | tf_op jit(solution)/shard_map/all_to_all | solution.py:214
  91.3 1.1 copy-start.1
  103.3 13.0 %copy-start.4 = (f32[16,8,128]{2,1,0:T(8,128)S(1)}, f32[16,8,128]{2,1,0:T(8,128)}, u32[]{:S(2)}) copy-start(f32[16,8,128]{2,1,0:T(8,128)} %fine.1) | copy-start | bytes 196612
  103.3 88.5 %all-to-all-start.1 = ((f32[512,1,768]{2,1,0:T(1,128)}), f32[512,1,768]{2,1,0:T(1,128)S(1)}, u32[]{:S(2)}, u32[]{:S(2)}) async-start(f32[512,1,768]{2,1,0:T(1,128)} %bitcast.18), calls=%async_computation.1 | async-start | bytes 3145728 | tf_op jit(solution)/shard_map/all_to_all | solution.py:214
  116.3 5.4 %collective-permute-start = (f32[16,8,128]{2,1,0:T(8,128)S(1)}, f32[16,8,128]{2,1,0:T(8,128)S(1)}, u32[]{:S(2)}, u32[]{:S(2)}) collective-permute-start(f32[16,8,128]{2,1,0:T(8,128)S(1)} %copy-done.4), channel_id=1, source_target_pairs={{0,1},{1,2},{2,3},{3,128},{128,129},{129,130},{130,131},{131,256},... | collective-permute-start | bytes 196616 | tf_op jit(solution)/shard_map/ppermute | solution.py:508
  119.7 6.3 %collective-permute-start.1 = (f32[16,8,128]{2,1,0:T(8,128)S(1)}, f32[16,8,128]{2,1,0:T(8,128)S(1)}, u32[]{:S(2)}, u32[]{:S(2)}) collective-permute-start(f32[16,8,128]{2,1,0:T(8,128)S(1)} %copy-done.4), channel_id=1, source_target_pairs={{1,0},{2,1},{3,2},{128,3},{129,128},{130,129},{131,130},{256,131},... | collective-permute-start | bytes 196616 | tf_op jit(solution)/shard_map/ppermute | solution.py:508
  126.1 58.7 %collective-permute-start.3 = (f32[8,24,128]{2,1,0:T(8,128)S(1)}, f32[8,24,128]{2,1,0:T(8,128)S(1)}, u32[]{:S(2)}, u32[]{:S(2)}) collective-permute-start(f32[8,24,128]{2,1,0:T(8,128)S(1)} %get-tuple-element.15), channel_id=1, source_target_pairs={{4,0},{8,4},{12,8},{16,12},{20,16},{24,20},{28,24},{32,28},{36,32}... | collective-permute-start | bytes 294920 | tf_op jit(solution)/shard_map/ppermute | solution.py:508
  129.0 55.7 %collective-permute-start.2 = (f32[8,24,128]{2,1,0:T(8,128)S(1)}, f32[8,24,128]{2,1,0:T(8,128)S(1)}, u32[]{:S(2)}, u32[]{:S(2)}) collective-permute-start(f32[8,24,128]{2,1,0:T(8,128)S(1)} %get-tuple-element.14), channel_id=1, source_target_pairs={{0,4},{4,8},{8,12},{12,16},{16,20},{20,24},{24,28},{28,32},{32,36}... | collective-permute-start | bytes 294920 | tf_op jit(solution)/shard_map/ppermute | solution.py:508
  191.8 1.2 copy-start
  232.5 22.1 %copy-start.3 = (f32[4,16,4,128]{3,2,1,0:T(4,128)}, f32[4,16,4,128]{3,2,1,0:T(4,128)S(1)}, u32[]{:S(2)}) copy-start(f32[4,16,4,128]{3,2,1,0:T(4,128)S(1)} %copy.15) | copy-start | bytes 393220
  232.5 14.7 %collective-permute-start.4 = (f32[4,64,128]{2,1,0:T(8,128)S(1)}, f32[4,64,128]{2,1,0:T(8,128)S(1)}, u32[]{:S(2)}, u32[]{:S(2)}) collective-permute-start(f32[4,64,128]{2,1,0:T(8,128)S(1)} %bitcast.30), channel_id=1, source_target_pairs={{0,8},{4,12},{8,16},{12,20},{16,24},{20,28},{24,32},{28,36},{32,40... | collective-permute-start | bytes 393224 | tf_op jit(solution)/shard_map/ppermute | solution.py:508
  235.9 11.3 %collective-permute-start.5 = (f32[4,64,128]{2,1,0:T(8,128)S(1)}, f32[4,64,128]{2,1,0:T(8,128)S(1)}, u32[]{:S(2)}, u32[]{:S(2)}) collective-permute-start(f32[4,64,128]{2,1,0:T(8,128)S(1)} %bitcast.31), channel_id=1, source_target_pairs={{0,4},{4,8},{8,12},{12,16},{16,20},{20,24},{24,28},{28,32},{32,36}... | collective-permute-start | bytes 393224 | tf_op jit(solution)/shard_map/ppermute | solution.py:508
  241.6 11.2 %collective-permute-start.6 = (f32[4,64,128]{2,1,0:T(8,128)S(1)}, f32[4,64,128]{2,1,0:T(8,128)S(1)}, u32[]{:S(2)}, u32[]{:S(2)}) collective-permute-start(f32[4,64,128]{2,1,0:T(8,128)S(1)} %bitcast.32), channel_id=1, source_target_pairs={{4,0},{8,4},{12,8},{16,12},{20,16},{24,20},{28,24},{32,28},{36,32}... | collective-permute-start | bytes 393224 | tf_op jit(solution)/shard_map/ppermute | solution.py:508
  243.6 11.1 %collective-permute-start.7 = (f32[4,64,128]{2,1,0:T(8,128)S(1)}, f32[4,64,128]{2,1,0:T(8,128)S(1)}, u32[]{:S(2)}, u32[]{:S(2)}) collective-permute-start(f32[4,64,128]{2,1,0:T(8,128)S(1)} %bitcast.33), channel_id=1, source_target_pairs={{8,0},{12,4},{16,8},{20,12},{24,16},{28,20},{32,24},{36,28},{40,32... | collective-permute-start | bytes 393224 | tf_op jit(solution)/shard_map/ppermute | solution.py:508
  247.2 7.4 %copy-start.9 = (f32[4,64,128]{2,1,0:T(8,128)}, f32[4,64,128]{2,1,0:T(8,128)S(1)}, u32[]{:S(2)}) copy-start(f32[4,64,128]{2,1,0:T(8,128)S(1)} %collective-permute-done.4.b0) | copy-start | bytes 393220
  247.3 7.4 %copy-start.10 = (f32[4,64,128]{2,1,0:T(8,128)}, f32[4,64,128]{2,1,0:T(8,128)S(1)}, u32[]{:S(2)}) copy-start(f32[4,64,128]{2,1,0:T(8,128)S(1)} %collective-permute-done.5.b1) | copy-start | bytes 393220
  252.9 1.8 copy-start.11
  254.6 0.6 copy-start.12
  289.5 18.3 %copy-start.2 = (f32[4,16,4,128]{3,2,1,0:T(4,128)}, f32[4,16,4,128]{3,2,1,0:T(4,128)S(1)}, u32[]{:S(2)}) copy-start(f32[4,16,4,128]{3,2,1,0:T(4,128)S(1)} %copy.17) | copy-start | bytes 393220
  289.5 18.3 %collective-permute-start.8 = (f32[4,64,128]{2,1,0:T(8,128)S(1)}, f32[4,64,128]{2,1,0:T(8,128)S(1)}, u32[]{:S(2)}, u32[]{:S(2)}) collective-permute-start(f32[4,64,128]{2,1,0:T(8,128)S(1)} %bitcast.23), channel_id=1, source_target_pairs={{0,8},{4,12},{8,16},{12,20},{16,24},{20,28},{24,32},{28,36},{32,40... | collective-permute-start | bytes 393224 | tf_op jit(solution)/shard_map/ppermute | solution.py:508
  294.8 13.0 %collective-permute-start.9 = (f32[4,64,128]{2,1,0:T(8,128)S(1)}, f32[4,64,128]{2,1,0:T(8,128)S(1)}, u32[]{:S(2)}, u32[]{:S(2)}) collective-permute-start(f32[4,64,128]{2,1,0:T(8,128)S(1)} %bitcast.24), channel_id=1, source_target_pairs={{0,4},{4,8},{8,12},{12,16},{16,20},{20,24},{24,28},{28,32},{32,36}... | collective-permute-start | bytes 393224 | tf_op jit(solution)/shard_map/ppermute | solution.py:508
  300.3 12.2 %collective-permute-start.10 = (f32[4,64,128]{2,1,0:T(8,128)S(1)}, f32[4,64,128]{2,1,0:T(8,128)S(1)}, u32[]{:S(2)}, u32[]{:S(2)}) collective-permute-start(f32[4,64,128]{2,1,0:T(8,128)S(1)} %bitcast.25), channel_id=1, source_target_pairs={{4,0},{8,4},{12,8},{16,12},{20,16},{24,20},{28,24},{32,28},{36,32}... | collective-permute-start | bytes 393224 | tf_op jit(solution)/shard_map/ppermute | solution.py:508
  302.2 11.2 %collective-permute-start.11 = (f32[4,64,128]{2,1,0:T(8,128)S(1)}, f32[4,64,128]{2,1,0:T(8,128)S(1)}, u32[]{:S(2)}, u32[]{:S(2)}) collective-permute-start(f32[4,64,128]{2,1,0:T(8,128)S(1)} %bitcast.26), channel_id=1, source_target_pairs={{8,0},{12,4},{16,8},{20,12},{24,16},{28,20},{32,24},{36,28},{40,32... | collective-permute-start | bytes 393224 | tf_op jit(solution)/shard_map/ppermute | solution.py:508
  307.8 5.6 %copy-start.5 = (f32[4,64,128]{2,1,0:T(8,128)}, f32[4,64,128]{2,1,0:T(8,128)S(1)}, u32[]{:S(2)}) copy-start(f32[4,64,128]{2,1,0:T(8,128)S(1)} %collective-permute-done.8.b0) | copy-start | bytes 393220
  307.8 5.6 %copy-start.6 = (f32[4,64,128]{2,1,0:T(8,128)}, f32[4,64,128]{2,1,0:T(8,128)S(1)}, u32[]{:S(2)}) copy-start(f32[4,64,128]{2,1,0:T(8,128)S(1)} %collective-permute-done.9.b1) | copy-start | bytes 393220
  312.4 1.0 copy-start.7
  313.4 0.7 copy-start.8

commit v2 on v1

--- a/solution.py
+++ b/solution.py
@@ -224,10 +224,11 @@
 
 XF = 32
 YF = 24
-X1 = 40
-Y1 = 64
-X2 = 20
-Y2 = 32
+X1 = 20
+Y1 = 32
+X2 = 10
+Y2 = 16
+HALF = 64
 STEP = 1.0 / 7.0
 
 
@@ -243,10 +244,10 @@
     return dot(first) + (dot(second) + dot(third))
 
 
-def over(count, body, per=4):
+def over(count, body, per=4, base=0):
     def group(t, carry):
         for k in range(per):
-            body(t * per + k)
+            body(base + t * per + k)
         return carry
 
     lax.fori_loop(0, count // per, group, 0)
@@ -275,6 +276,9 @@
         self.low = jnp.where(lane == 0, 0.0, 1.0)
         self.high = jnp.where(lane == LANES - 1, 0.0, 1.0)
 
+    def scale(self, x):
+        return self.mask * inside(self.first + x, self.count)
+
     def around(self, ref, x):
         c = ref[x + 1]
         near = ref[x] + ref[x + 2]
@@ -284,31 +288,42 @@
 
 
 class Coarse:
-    def __init__(self, first, count, x, y, z):
+    def __init__(self, first, count, x, y, first_y, count_y, z):
         self.first = first
         self.count = count
         self.x = x
+        row = rows_of(y) + first_y
+        lane = lanes_of(y)
         self.y = y
-        self.mask = jnp.where(lanes_of(y) < z, STEP, 0.0)
-        row = rows_of(y)
-        self.low = jnp.where(row == 0, 0.0, 1.0)
-        self.high = jnp.where(row == y - 1, 0.0, 1.0)
+        self.left = lane < HALF
+        place = lane % HALF
+        self.mask = jnp.where((place < z) & (row >= 0) & (row < count_y), STEP, 0.0)
+        self.low = jnp.where(place == 0, 0.0, 1.0)
+        self.high = jnp.where(place == HALF - 1, 0.0, 1.0)
+
+    def scale(self, x):
+        here = inside(self.first + x, self.count)
+        there = inside(self.first + self.x + x, self.count)
+        return self.mask * jnp.where(self.left, here, there)
 
     def around(self, ref, x):
         c = ref[x + 1]
         near = ref[x] + ref[x + 2]
-        near = near + (pltpu.roll(c, 1, 0) * self.low + pltpu.roll(c, self.y - 1, 0) * self.high)
-        near = near + (pltpu.roll(c, 1, 1) + pltpu.roll(c, LANES - 1, 1))
+        near = near + (pltpu.roll(c, 1, 0) + pltpu.roll(c, self.y - 1, 0))
+        near = near + (pltpu.roll(c, 1, 1) * self.low + pltpu.roll(c, LANES - 1, 1) * self.high)
         return c, near
 
-
-def sweep(level, source, right, shift, target):
+    def join(self, ref):
+        ref[0] = jnp.where(self.left, 0.0, pltpu.roll(ref[self.x], HALF, 1))
+        ref[self.x + 1] = jnp.where(self.left, pltpu.roll(ref[1], HALF, 1), 0.0)
+
+
+def sweep(level, source, right, target, per=4, base=0, count=None):
     def body(x):
         c, near = level.around(source, x)
-        scale = inside(level.first + x, level.count)
-        target[x + 1] = (right[x + shift] + (c + near)) * (level.mask * scale)
-
-    over(level.x, body)
+        target[x + 1] = (right[x] + (c + near)) * level.scale(x)
+
+    over(level.x if count is None else count, body, per, base)
 
 
 def clear(ref, size):
@@ -347,35 +362,34 @@
         c, around = level.around(wide, x)
         edge = c * ((1.0 - level.low) + (1.0 - level.high))
         value = 2.0 * fine[x] - (6.0 * c - (around + edge))
-        scale = inside(level.first + x, level.count)
-        held = jnp.where(level.mask * scale > 0.0, value, 0.0)
+        held = jnp.where(level.scale(x) > 0.0, value, 0.0)
         resid[x] = held
         first[x + 1] = held * STEP
 
     over(XF, body)
-    sweep(level, first, resid, 0, second)
+    sweep(level, first, resid, second)
     corr[...] = second[1 : XF + 1]
     lower_of(level, second, resid, strip, pairs[...], lower)
 
 
-def coarse(pos, blocks, corr, resid, pairs, spread, one, scratch):
+def coarse(pos, blocks, corr, resid, tables, scratch):
     right1, left1, other1, right2, left2, other2, rows, double, grown, twice, first, second = scratch
-    level1 = Coarse(8 * pos[0] - 16, 256, X1, Y1, 64)
-    level2 = Coarse(4 * pos[0] - 8, 128, X2, Y2, 32)
+    spread, merge, widen = tables
+    level1 = Coarse(8 * pos[0] - 16, 256, X1, Y1, 4 * pos[1] - 14, 64, HALF)
+    level2 = Coarse(4 * pos[0] - 8, 128, X2, Y2, 2 * pos[1] - 7, 32, HALF // 2)
     fine = Fine(pos)
-    lane = lanes_of(Y1)
-    for ref in (left1, other1):
-        clear(ref, X1)
-    for ref in (left2, other2):
-        clear(ref, X2)
-    for b, block in enumerate(blocks):
-        for xx in range(4):
-            value = block[xx]
-            for half in range(2):
-                held = jnp.where(lane < 64, pltpu.roll(value, 64, 1) if half else value, 0.0)
-                right1[b * 8 + half * 4 + xx] = held
-                left1[1 + b * 8 + half * 4 + xx] = held * STEP
-    sweep(level1, left1, right1, 0, other1)
+    for x in range(X1):
+        here = blocks[x // 8][x % 4]
+        there = blocks[(x + X1) // 8][x % 4]
+        if (x % 8) // 4:
+            value = pltpu.roll(jnp.where(level1.left, there, here), HALF, 1)
+        else:
+            value = jnp.where(level1.left, here, there)
+        right1[x] = value
+        left1[x + 1] = value * STEP
+    level1.join(left1)
+    sweep(level1, left1, right1, other1)
+    level1.join(other1)
 
     def down(k):
         total = None
@@ -387,20 +401,22 @@
         rows[pl.ds(pl.multiple_of(k * Y2, Y2), Y2), :] = double[pl.ds(0, Y2, stride=2), :] + double[pl.ds(1, Y2, stride=2), :]
 
     over(X2, down, 1)
-    rows[...] = exact(rows[...], pairs)
+    rows[...] = exact(rows[...], merge)
 
     def begin(k):
         value = rows[pl.ds(pl.multiple_of(k * Y2, Y2), Y2), :]
-        scale = inside(level2.first + k, level2.count)
-        value = jnp.where(level2.mask * scale > 0.0, 0.5 * value, 0.0)
+        value = jnp.where(level2.scale(k) > 0.0, 0.5 * value, 0.0)
         right2[k] = value
         left2[k + 1] = value * STEP
 
-    over(X2, begin)
-    sweep(level2, left2, right2, 0, other2)
-    sweep(level2, other2, right2, 0, left2)
-    sweep(level2, left2, right2, 0, other2)
-    rows[...] = exact(other2[1 : X2 + 1].reshape(X2 * Y2, LANES), spread)
+    over(X2, begin, 5)
+    level2.join(left2)
+    sweep(level2, left2, right2, other2, 5)
+    level2.join(other2)
+    sweep(level2, other2, right2, left2, 5)
+    level2.join(left2)
+    sweep(level2, left2, right2, other2, 5)
+    rows[...] = exact(other2[1 : X2 + 1].reshape(X2 * Y2, LANES), widen)
 
     def up(k):
         value = rows[pl.ds(pl.multiple_of(k * Y2, Y2), Y2), :]
@@ -411,40 +427,46 @@
         other1[2 + 2 * k] = other1[2 + 2 * k] + value
 
     over(X2, up, 1)
-    sweep(level1, other1, right1, 0, left1)
-    sweep(level1, left1, right1, 0, other1)
-    amount = 124 - 4 * pos[1]
+    level1.join(other1)
+    sweep(level1, other1, right1, left1)
+    level1.join(left1)
+    sweep(level1, left1, right1, other1)
     for k in range(16):
-        value = other1[13 + k]
-        value = jnp.concatenate([jnp.zeros((8, LANES), F32), value, jnp.zeros((56, LANES), F32)], axis=0)
-        grown[k * 16 : k * 16 + 16, :] = pltpu.roll(value, amount, 0)[0:16]
+        x = 12 + k
+        value = other1[1 + x % X1][10:26]
+        grown[k * 16 : k * 16 + 16, :] = value if x < X1 else pltpu.roll(value, HALF, 1)
     grown[...] = exact(grown[...], spread)
-    clear(first, XF)
-    clear(second, XF)
     for i in range(16):
         value = grown[i * 16 : i * 16 + 12, :]
         twice[pl.ds(0, 12, stride=2), :] = value
         twice[pl.ds(1, 12, stride=2), :] = value
         first[1 + 2 * i] = corr[2 * i] + twice[...]
         first[2 + 2 * i] = corr[2 * i + 1] + twice[...]
-    sweep(fine, first, resid, 0, second)
-    sweep(fine, second, resid, 0, first)
     return fine
 
 
-def turn_kernel(pos, b0, b1, b2, b3, b4, corr, resid, pairs, spread, after, lower, *scratch):
+def turn_kernel(pos, b0, b1, b2, b3, b4, corr, resid, pairs, spread, merge, widen, after, lower, *scratch):
     strip, scratch = scratch[-1], scratch[:-1]
-    fine = coarse(pos, (b0, b1, b2, b3, b4), corr, resid, pairs[...], spread[...], None, scratch)
+    tables = (spread[...], merge[...], widen[...])
+    fine = coarse(pos, (b0, b1, b2, b3, b4), corr, resid, tables, scratch)
     first, second = scratch[-2:]
-    sweep(fine, first, resid, 0, second)
-    sweep(fine, second, resid, 0, first)
-    after[...] = first[1 : XF + 1]
+    sweep(fine, first, resid, second, 2, 3, 26)
+    sweep(fine, second, resid, first, 4, 4, 24)
+    sweep(fine, first, resid, second, 2, 5, 22)
+    sweep(fine, second, resid, first, 4, 6, 20)
+    for k in range(6, 26):
+        after[k] = first[k + 1]
+    for k in (0, 1, 2, 3, 4, 5, 26, 27, 28, 29, 30, 31):
+        after[k] = jnp.zeros((YF, LANES), F32)
     lower_of(fine, first, resid, strip, pairs[...], lower)
 
 
-def close_kernel(pos, b0, b1, b2, b3, b4, corr, resid, pairs, spread, start, out, *scratch):
-    coarse(pos, (b0, b1, b2, b3, b4), corr, resid, pairs[...], spread[...], None, scratch)
-    first = scratch[-2]
+def close_kernel(pos, b0, b1, b2, b3, b4, corr, resid, spread, merge, widen, start, out, *scratch):
+    tables = (spread[...], merge[...], widen[...])
+    fine = coarse(pos, (b0, b1, b2, b3, b4), corr, resid, tables, scratch)
+    first, second = scratch[-2:]
+    sweep(fine, first, resid, second, 2, 7, 18)
+    sweep(fine, second, resid, first, 4, 8, 16)
     for k in range(16):
         out[k] = start[k] + first[9 + k][8:16]
 
@@ -493,14 +515,14 @@
     return many(open_kernel, "opening", 4, shapes, scratch)(pos, near, fine, pairs, spread)
 
 
-def turning(pos, blocks, corr, resid, pairs, spread):
+def turning(pos, blocks, corr, resid, tables):
     shapes = [shaped(XF, YF, LANES), shaped(16, LANES)]
-    return many(turn_kernel, "turning", 9, shapes, inner() + [held(64, LANES)])(pos, *blocks, corr, resid, pairs, spread)
-
-
-def closing(pos, blocks, corr, resid, pairs, spread, start):
-    return many(close_kernel, "closing", 10, [shaped(16, 8, LANES)], inner())(
-        pos, *blocks, corr, resid, pairs, spread, start
+    return many(turn_kernel, "turning", 11, shapes, inner() + [held(64, LANES)])(pos, *blocks, corr, resid, *tables)
+
+
+def closing(pos, blocks, corr, resid, tables, start):
+    return many(close_kernel, "closing", 11, [shaped(16, 8, LANES)], inner())(
+        pos, *blocks, corr, resid, *tables[1:], start
     )[0]
 
 
@@ -508,10 +530,12 @@
     return lax.ppermute(value, axes, [(i, i + step) for i in range(size) if 0 <= i + step < size])
 
 
-def gather(lower):
+def gather(lower, place):
     every = jnp.broadcast_to(lower[None], (YY, 16, LANES))
     every = lax.all_to_all(every, ("group", "gy"), 0, 0, tiled=True)
-    block = every.reshape(YY, 4, 4, LANES).transpose(1, 0, 2, 3).reshape(4, Y1, LANES)
+    every = jnp.pad(every, ((4, 4), (0, 0), (0, 0)))
+    window = lax.dynamic_slice(every, (place, 0, 0), (9, 16, LANES))
+    block = window.reshape(9, 4, 4, LANES).transpose(1, 0, 2, 3).reshape(4, 36, LANES)[:, 2:34]
     return [block if step == 0 else shifted(block, "gx", GX, step) for step in (2, 1, 0, -1, -2)]
 
 
@@ -526,6 +550,10 @@
 def local(parent_mass, fine_mass, offsets):
     high, low, pairs, column, row, eigen = constants()
     spread = pairs.T
+    spot = np.arange(LANES)
+    merge = np.zeros((LANES, LANES), np.float32)
+    merge[spot, spot % HALF // 2 + HALF * (spot // HALF)] = 1.0
+    tables = (pairs, spread, jnp.asarray(merge, BF16), jnp.asarray(merge.T, BF16))
     pos = jnp.stack([lax.axis_index("gx"), lax.axis_index(("group", "gy"))]).astype(jnp.int32)
     wave = lax.dynamic_slice(eigen, (lax.axis_index(ALL),), (1,))
     wide = widened(fine_mass)
@@ -534,8 +562,8 @@
     near = near_back(offsets, got, high, low)
     start, resid, corr, lower = opening(pos, near, wide, pairs, spread)
     potential = whole_back(got, high, low)
-    corr, lower = turning(pos, gather(lower), corr, resid, pairs, spread)
-    out = closing(pos, gather(lower), corr, resid, pairs, spread, start)
+    corr, lower = turning(pos, gather(lower, pos[1]), corr, resid, tables)
+    out = closing(pos, gather(lower, pos[1]), corr, resid, tables, start)
     return (potential.reshape(WX, WY, NP), out)
 
 

time: 328 us -> 316 us (0.963)
  the two profiles are of different devices: /device:TPU:120 before, /device:TPU:112 now
where the time goes in v2:
time: 316 us; the launch traced here: 315 us
  waiting for transfers between devices  149 us (47%)
  starting transfers between devices  93.3 us (30%)
  Pallas kernels  43.5 us (14%)
  blocking collectives  20.5 us (6%)
  local copies, waits for them, and re-layouts  6.98 us (2%)
    all_to_all x2, waiting for transfers between devices, swap(): lax.all_to_all(piece, ALL, 0, 0, tiled=True)  117 us
    ppermute x12, starting transfers between devices, shifted(): lax.ppermute(value, axes, [(i, i + step) for i in range(size) if 0 <= i +...  41.3 us
    all_to_all x2, starting transfers between devices, swap(): lax.all_to_all(piece, ALL, 0, 0, tiled=True)  35.2 us
    all_to_all x1, blocking collectives, gather(): every = lax.all_to_all(every, ('group', 'gy'), 0, 0, tiled=True)  20.5 us
    all_to_all x1, starting transfers between devices, gather(): every = lax.all_to_all(every, ('group', 'gy'), 0, 0, tiled=True)  16.8 us
    all_to_all x1, waiting for transfers between devices, gather(): every = lax.all_to_all(every, ('group', 'gy'), 0, 0, tiled=True)  16.5 us
    ppermute x12, waiting for transfers between devices, shifted(): lax.ppermute(value, axes, [(i, i + step) for i in range(size) if 0 <= i +...  15.5 us
    pallas_call x1, Pallas kernels, spectral(): call(plane_kernel, 'plane', [SMEM, SMEM] + [VMEM] * 5, (NP * BACK, LANES)...  11 us
  transfers between devices with their start and end apart: 15, of which 9 were waited for; matrix products, arithmetic and copies ran while one was open for 1% of the time, Pallas kernels for 1%

profile of v2, /device:TPU:112, one launch (start us, length us, event | category | flops | bytes accessed | tf_op | source)
XLA Modules:
  0.0 315.2 jit_solution(10277897917191782501)
XLA Ops:
  0.6 4.1 %forward.1 = f32[2560,128]{1,0:T(8,128)} custom-call(s32[3]{0:T(128)} %offsets.5, f32[512,512]{1,0:T(8,128)} %bitcast.22, f32[16,8,128]{2,1,0:T(8,128)} %fine.1, bf16[512,512]{1,0:T(8,128)(2,1)} %constant.54.high, bf16[512,512]{1,0:T(8,128)(2,1)} %constant.57.low, bf16[128,128]{1,0:T(8,128)(2,1)} %constant.42.clone.pairs), custom_call_target="tpu_custom_call" | custom-call | tf_op jit(solution)/shard_map/forward/pallas_call | solution.py:189
  4.7 22.6 %all-to-all-start = ((f32[512,1,640]{2,1,0:T(1,128)}), f32[512,1,640]{2,1,0:T(1,128)S(1)}, u32[]{:S(2)}, u32[]{:S(2)}) async-start(f32[512,1,640]{2,1,0:T(1,128)} %bitcast.20), calls=%async_computation | async-start | bytes 2621440 | tf_op jit(solution)/shard_map/all_to_all | solution.py:214
  27.3 1.3 dynamic_slice.9.wave
  28.6 63.1 %all-to-all-done = f32[512,1,640]{2,1,0:T(1,128)S(1)} async-done(((f32[512,1,640]{2,1,0:T(1,128)}), f32[512,1,640]{2,1,0:T(1,128)S(1)}, u32[]{:S(2)}, u32[]{:S(2)}) %all-to-all-start) | async-done | bytes 1310752 | tf_op jit(solution)/shard_map/all_to_all | solution.py:214
  91.6 1.1 copy-done.1
  92.7 11.0 %plane.1 = f32[3072,128]{1,0:T(8,128)} custom-call(s32[3]{0:T(128)} %offsets.5, f32[1]{0:T(128)} %dynamic_slice.9.wave, f32[2560,128]{1,0:T(8,128)} %bitcast.19, bf16[512,512]{1,0:T(8,128)(2,1)} %constant.54.high, bf16[512,512]{1,0:T(8,128)(2,1)} %constant.57.low, f32[512,1]{1,0:T(8,128)} %constant.43.clone.column, f32[1,512]{1,0:T(1,128)} %constant.44.clone.row), custom_call_target="tpu_custom_call" | custom-call | tf_op jit(solution)/shard_map/plane/pallas_call | solution.py:195
  103.7 12.7 %all-to-all-start.1 = ((f32[512,1,768]{2,1,0:T(1,128)}), f32[512,1,768]{2,1,0:T(1,128)S(1)}, u32[]{:S(2)}, u32[]{:S(2)}) async-start(f32[512,1,768]{2,1,0:T(1,128)} %bitcast.18), calls=%async_computation.1 | async-start | bytes 3145728 | tf_op jit(solution)/shard_map/all_to_all | solution.py:214
  116.3 3.4 %collective-permute-start = (f32[16,8,128]{2,1,0:T(8,128)S(1)}, f32[16,8,128]{2,1,0:T(8,128)S(1)}, u32[]{:S(2)}, u32[]{:S(2)}) collective-permute-start(f32[16,8,128]{2,1,0:T(8,128)S(1)} %copy-done.2), channel_id=1, source_target_pairs={{0,1},{1,2},{2,3},{3,128},{128,129},{129,130},{130,131},{131,256},... | collective-permute-start | bytes 196616 | tf_op jit(solution)/shard_map/ppermute | solution.py:530
  119.7 1.3 collective-permute-start.1
  121.0 0.7 collective-permute-done
  121.7 4.4 %collective-permute-done.1 = f32[16,8,128]{2,1,0:T(8,128)S(1)} collective-permute-done((f32[16,8,128]{2,1,0:T(8,128)S(1)}, f32[16,8,128]{2,1,0:T(8,128)S(1)}, u32[]{:S(2)}, u32[]{:S(2)}) %collective-permute-start.1) | collective-permute-done | bytes 65568 | tf_op jit(solution)/shard_map/ppermute | solution.py:530
  126.2 3.2 %collective-permute-start.2 = (f32[8,24,128]{2,1,0:T(8,128)S(1)}, f32[8,24,128]{2,1,0:T(8,128)S(1)}, u32[]{:S(2)}, u32[]{:S(2)}) collective-permute-start(f32[8,24,128]{2,1,0:T(8,128)S(1)} %get-tuple-element.14), channel_id=1, source_target_pairs={{0,4},{4,8},{8,12},{12,16},{16,20},{20,24},{24,28},{28,32},{32,36}... | collective-permute-start | bytes 294920 | tf_op jit(solution)/shard_map/ppermute | solution.py:530
  129.4 2.8 collective-permute-start.3
  132.2 0.6 pad_add_fusion.pos
  132.8 0.2 collective-permute-done.2
  133.0 3.8 %collective-permute-done.3 = f32[8,24,128]{2,1,0:T(8,128)S(1)} collective-permute-done((f32[8,24,128]{2,1,0:T(8,128)S(1)}, f32[8,24,128]{2,1,0:T(8,128)S(1)}, u32[]{:S(2)}, u32[]{:S(2)}) %collective-permute-start.3) | collective-permute-done | bytes 98336 | tf_op jit(solution)/shard_map/ppermute | solution.py:530
  136.8 0.8 pad_maximum_fusion.fine
  137.6 53.5 %all-to-all-done.1 = f32[512,1,768]{2,1,0:T(1,128)S(1)} async-done(((f32[512,1,768]{2,1,0:T(1,128)}), f32[512,1,768]{2,1,0:T(1,128)S(1)}, u32[]{:S(2)}, u32[]{:S(2)}) %all-to-all-start.1) | async-done | bytes 1572896 | tf_op jit(solution)/shard_map/all_to_all | solution.py:214
  191.1 1.2 copy-done
  192.2 3.1 near.1
  195.3 4.0 %opening.1 = (f32[16,8,128]{2,1,0:T(8,128)}, f32[32,24,128]{2,1,0:T(8,128)}, f32[32,24,128]{2,1,0:T(8,128)}, f32[16,128]{1,0:T(8,128)}) custom-call(s32[2]{0:T(128)} %pad_add_fusion.pos, f32[256,128]{1,0:T(8,128)} %near.1, f32[32,24,128]{2,1,0:T(8,128)} %pad_maximum_fusion.fine, bf16[128,128]{1,0:T(8,128)(2,1)} %constant.42.clone.pairs, ...), custom_call_target="tpu_custom_call" | custom-call | tf_op jit(solution)/shard_map/opening/pallas_call | solution.py:515
  199.3 1.4 broadcast_in_dim.4
  200.7 16.8 %all-to-all-start.2 = ((f32[16,16,128]{2,1,0:T(8,128)}), f32[16,16,128]{2,1,0:T(8,128)S(1)}, u32[]{:S(2)}, u32[]{:S(2)}) async-start(f32[16,16,128]{2,1,0:T(8,128)} %broadcast_in_dim.4), calls=%async_computation.2 | async-start | bytes 262144 | tf_op jit(solution)/shard_map/all_to_all | solution.py:535
  217.4 16.5 %all-to-all-done.2 = f32[16,16,128]{2,1,0:T(8,128)S(1)} async-done(((f32[16,16,128]{2,1,0:T(8,128)}), f32[16,16,128]{2,1,0:T(8,128)S(1)}, u32[]{:S(2)}, u32[]{:S(2)}) %all-to-all-start.2) | async-done | bytes 131104 | tf_op jit(solution)/shard_map/all_to_all | solution.py:535
  234.0 4.4 %collective-permute-start.4 = (f32[4,32,128]{2,1,0:T(8,128)S(1)}, f32[4,32,128]{2,1,0:T(8,128)S(1)}, u32[]{:S(2)}, u32[]{:S(2)}) collective-permute-start(f32[4,32,128]{2,1,0:T(8,128)S(1)} %copy.22.b2), channel_id=1, source_target_pairs={{0,8},{4,12},{8,16},{12,20},{16,24},{20,28},{24,32},{28,36},{32,40... | collective-permute-start | bytes 196616 | tf_op jit(solution)/shard_map/ppermute | solution.py:530
  238.4 4.5 %collective-permute-start.5 = (f32[4,32,128]{2,1,0:T(8,128)S(1)}, f32[4,32,128]{2,1,0:T(8,128)S(1)}, u32[]{:S(2)}, u32[]{:S(2)}) collective-permute-start(f32[4,32,128]{2,1,0:T(8,128)S(1)} %copy.22.b2), channel_id=1, source_target_pairs={{0,4},{4,8},{8,12},{12,16},{16,20},{20,24},{24,28},{28,32},{32,36}... | collective-permute-start | bytes 196616 | tf_op jit(solution)/shard_map/ppermute | solution.py:530
  242.8 2.3 collective-permute-start.6
  245.2 4.2 %collective-permute-start.7 = (f32[4,32,128]{2,1,0:T(8,128)S(1)}, f32[4,32,128]{2,1,0:T(8,128)S(1)}, u32[]{:S(2)}, u32[]{:S(2)}) collective-permute-start(f32[4,32,128]{2,1,0:T(8,128)S(1)} %copy.22.b2), channel_id=1, source_target_pairs={{8,0},{12,4},{16,8},{20,12},{24,16},{28,20},{32,24},{36,28},{40,32... | collective-permute-start | bytes 196616 | tf_op jit(solution)/shard_map/ppermute | solution.py:530
  249.4 0.0 copy-start.8
  249.4 0.0 collective-permute-done.5.b1
  249.4 0.0 copy-start.10
  249.4 0.3 collective-permute-done.6.b3
  249.7 6.1 %collective-permute-done.7.b4 = f32[4,32,128]{2,1,0:T(8,128)S(1)} collective-permute-done((f32[4,32,128]{2,1,0:T(8,128)S(1)}, f32[4,32,128]{2,1,0:T(8,128)S(1)}, u32[]{:S(2)}, u32[]{:S(2)}) %collective-permute-start.7) | collective-permute-done | bytes 65568 | tf_op jit(solution)/shard_map/ppermute | solution.py:530
  255.8 0.6 copy-done.12
  256.4 10.1 %turning.1 = (f32[32,24,128]{2,1,0:T(8,128)}, f32[16,128]{1,0:T(8,128)}) custom-call(s32[2]{0:T(128)} %pad_add_fusion.pos, f32[4,32,128]{2,1,0:T(8,128)} %copy-done.8, f32[4,32,128]{2,1,0:T(8,128)} %copy-done.10, f32[4,32,128]{2,1,0:T(8,128)} %copy-done.4, f32[4,32,128]{2,1,0:T(8,128)} %copy-done.11, f32[4,32,128]{2,1,0:T(8,128)} %copy-done.12, ...), custom_call_target="tpu_custom_call" | custom-call | tf_op jit(solution)/shard_map/turning/pallas_call | solution.py:520
  266.5 0.7 broadcast_in_dim.5
  267.2 20.5 %all_to_all.20 = f32[16,16,128]{2,1,0:T(8,128)S(1)} all-to-all(f32[16,16,128]{2,1,0:T(8,128)S(1)} %broadcast_in_dim.5), channel_id=1, replica_groups=mesh['group'=4,'gx'=32,'gy'=4] {'group','gy'}, dimensions={0} | all-to-all | bytes 262144 | tf_op jit(solution)/shard_map/all_to_all | solution.py:535
  287.8 1.9 collective-permute-start.10
  289.7 1.9 collective-permute-start.11
  291.6 7.5 %collective-permute-start.8 = (f32[4,32,128]{2,1,0:T(8,128)S(1)}, f32[4,32,128]{2,1,0:T(8,128)S(1)}, u32[]{:S(2)}, u32[]{:S(2)}) collective-permute-start(f32[4,32,128]{2,1,0:T(8,128)S(1)} %copy.23.b2), channel_id=1, source_target_pairs={{0,8},{4,12},{8,16},{12,20},{16,24},{20,28},{24,32},{28,36},{32,40... | collective-permute-start | bytes 196616 | tf_op jit(solution)/shard_map/ppermute | solution.py:530
  299.2 3.9 %collective-permute-start.9 = (f32[4,32,128]{2,1,0:T(8,128)S(1)}, f32[4,32,128]{2,1,0:T(8,128)S(1)}, u32[]{:S(2)}, u32[]{:S(2)}) collective-permute-start(f32[4,32,128]{2,1,0:T(8,128)S(1)} %copy.23.b2), channel_id=1, source_target_pairs={{0,4},{4,8},{8,12},{12,16},{16,20},{20,24},{24,28},{28,32},{32,36}... | collective-permute-start | bytes 196616 | tf_op jit(solution)/shard_map/ppermute | solution.py:530
  303.1 3.7 %whole.1 = f32[512,512]{1,0:T(8,128)} custom-call(f32[3072,128]{1,0:T(8,128)} %bitcast.17, bf16[512,512]{1,0:T(8,128)(2,1)} %constant.54.high, bf16[512,512]{1,0:T(8,128)(2,1)} %constant.57.low), custom_call_target="tpu_custom_call" | custom-call | tf_op jit(solution)/shard_map/whole/pallas_call | solution.py:209
  306.8 0.0 collective-permute-done.10.b3
  306.9 0.6 copy-done.5
  307.4 0.0 copy-done.6
  307.4 0.0 copy-done.7
  307.5 0.0 copy-done.9
  307.5 7.7 %closing.1 = f32[16,8,128]{2,1,0:T(8,128)} custom-call(s32[2]{0:T(128)} %pad_add_fusion.pos, f32[4,32,128]{2,1,0:T(8,128)} %copy-done.7, f32[4,32,128]{2,1,0:T(8,128)} %copy-done.9, f32[4,32,128]{2,1,0:T(8,128)} %copy-done.3, f32[4,32,128]{2,1,0:T(8,128)} %copy-done.5, f32[4,32,128]{2,1,0:T(8,128)} %copy-done.6, f32[32,24,128]{2,1,0:T(8,128)} %get-tuple-element.12.corr, ...), custom_call_target="tpu_custom_call" | custom-call | tf_op jit(solution)/shard_map/closing/pallas_call | solution.py:524
  (33 shorter events, 0.2 us)
Async XLA Ops:
  4.7 86.9 %all-to-all-start = ((f32[512,1,640]{2,1,0:T(1,128)}), f32[512,1,640]{2,1,0:T(1,128)S(1)}, u32[]{:S(2)}, u32[]{:S(2)}) async-start(f32[512,1,640]{2,1,0:T(1,128)} %bitcast.20), calls=%async_computation | async-start | bytes 2621440 | tf_op jit(solution)/shard_map/all_to_all | solution.py:214
  91.6 1.1 copy-start.1
  103.7 12.7 %copy-start.2 = (f32[16,8,128]{2,1,0:T(8,128)S(1)}, f32[16,8,128]{2,1,0:T(8,128)}, u32[]{:S(2)}) copy-start(f32[16,8,128]{2,1,0:T(8,128)} %fine.1) | copy-start | bytes 196612
  103.7 87.4 %all-to-all-start.1 = ((f32[512,1,768]{2,1,0:T(1,128)}), f32[512,1,768]{2,1,0:T(1,128)S(1)}, u32[]{:S(2)}, u32[]{:S(2)}) async-start(f32[512,1,768]{2,1,0:T(1,128)} %bitcast.18), calls=%async_computation.1 | async-start | bytes 3145728 | tf_op jit(solution)/shard_map/all_to_all | solution.py:214
  116.3 5.4 %collective-permute-start = (f32[16,8,128]{2,1,0:T(8,128)S(1)}, f32[16,8,128]{2,1,0:T(8,128)S(1)}, u32[]{:S(2)}, u32[]{:S(2)}) collective-permute-start(f32[16,8,128]{2,1,0:T(8,128)S(1)} %copy-done.2), channel_id=1, source_target_pairs={{0,1},{1,2},{2,3},{3,128},{128,129},{129,130},{130,131},{131,256},... | collective-permute-start | bytes 196616 | tf_op jit(solution)/shard_map/ppermute | solution.py:530
  119.7 6.4 %collective-permute-start.1 = (f32[16,8,128]{2,1,0:T(8,128)S(1)}, f32[16,8,128]{2,1,0:T(8,128)S(1)}, u32[]{:S(2)}, u32[]{:S(2)}) collective-permute-start(f32[16,8,128]{2,1,0:T(8,128)S(1)} %copy-done.2), channel_id=1, source_target_pairs={{1,0},{2,1},{3,2},{128,3},{129,128},{130,129},{131,130},{256,131},... | collective-permute-start | bytes 196616 | tf_op jit(solution)/shard_map/ppermute | solution.py:530
  126.2 6.8 %collective-permute-start.2 = (f32[8,24,128]{2,1,0:T(8,128)S(1)}, f32[8,24,128]{2,1,0:T(8,128)S(1)}, u32[]{:S(2)}, u32[]{:S(2)}) collective-permute-start(f32[8,24,128]{2,1,0:T(8,128)S(1)} %get-tuple-element.14), channel_id=1, source_target_pairs={{0,4},{4,8},{8,12},{12,16},{16,20},{20,24},{24,28},{28,32},{32,36}... | collective-permute-start | bytes 294920 | tf_op jit(solution)/shard_map/ppermute | solution.py:530
  129.4 7.3 %collective-permute-start.3 = (f32[8,24,128]{2,1,0:T(8,128)S(1)}, f32[8,24,128]{2,1,0:T(8,128)S(1)}, u32[]{:S(2)}, u32[]{:S(2)}) collective-permute-start(f32[8,24,128]{2,1,0:T(8,128)S(1)} %get-tuple-element.15), channel_id=1, source_target_pairs={{4,0},{8,4},{12,8},{16,12},{20,16},{24,20},{28,24},{32,28},{36,32}... | collective-permute-start | bytes 294920 | tf_op jit(solution)/shard_map/ppermute | solution.py:530
  191.1 1.2 copy-start
  200.7 33.3 %all-to-all-start.2 = ((f32[16,16,128]{2,1,0:T(8,128)}), f32[16,16,128]{2,1,0:T(8,128)S(1)}, u32[]{:S(2)}, u32[]{:S(2)}) async-start(f32[16,16,128]{2,1,0:T(8,128)} %broadcast_in_dim.4), calls=%async_computation.2 | async-start | bytes 262144 | tf_op jit(solution)/shard_map/all_to_all | solution.py:535
  234.0 21.8 %copy-start.4 = (f32[4,32,128]{2,1,0:T(8,128)}, f32[4,32,128]{2,1,0:T(8,128)S(1)}, u32[]{:S(2)}) copy-start(f32[4,32,128]{2,1,0:T(8,128)S(1)} %copy.22.b2) | copy-start | bytes 196612
  234.0 15.3 %collective-permute-start.4 = (f32[4,32,128]{2,1,0:T(8,128)S(1)}, f32[4,32,128]{2,1,0:T(8,128)S(1)}, u32[]{:S(2)}, u32[]{:S(2)}) collective-permute-start(f32[4,32,128]{2,1,0:T(8,128)S(1)} %copy.22.b2), channel_id=1, source_target_pairs={{0,8},{4,12},{8,16},{12,20},{16,24},{20,28},{24,32},{28,36},{32,40... | collective-permute-start | bytes 196616 | tf_op jit(solution)/shard_map/ppermute | solution.py:530
  238.4 11.0 %collective-permute-start.5 = (f32[4,32,128]{2,1,0:T(8,128)S(1)}, f32[4,32,128]{2,1,0:T(8,128)S(1)}, u32[]{:S(2)}, u32[]{:S(2)}) collective-permute-start(f32[4,32,128]{2,1,0:T(8,128)S(1)} %copy.22.b2), channel_id=1, source_target_pairs={{0,4},{4,8},{8,12},{12,16},{16,20},{20,24},{24,28},{28,32},{32,36}... | collective-permute-start | bytes 196616 | tf_op jit(solution)/shard_map/ppermute | solution.py:530
  242.8 6.8 %collective-permute-start.6 = (f32[4,32,128]{2,1,0:T(8,128)S(1)}, f32[4,32,128]{2,1,0:T(8,128)S(1)}, u32[]{:S(2)}, u32[]{:S(2)}) collective-permute-start(f32[4,32,128]{2,1,0:T(8,128)S(1)} %copy.22.b2), channel_id=1, source_target_pairs={{4,0},{8,4},{12,8},{16,12},{20,16},{24,20},{28,24},{32,28},{36,32}... | collective-permute-start | bytes 196616 | tf_op jit(solution)/shard_map/ppermute | solution.py:530
  245.2 10.6 %collective-permute-start.7 = (f32[4,32,128]{2,1,0:T(8,128)S(1)}, f32[4,32,128]{2,1,0:T(8,128)S(1)}, u32[]{:S(2)}, u32[]{:S(2)}) collective-permute-start(f32[4,32,128]{2,1,0:T(8,128)S(1)} %copy.22.b2), channel_id=1, source_target_pairs={{8,0},{12,4},{16,8},{20,12},{24,16},{28,20},{32,24},{36,28},{40,32... | collective-permute-start | bytes 196616 | tf_op jit(solution)/shard_map/ppermute | solution.py:530
  249.4 6.4 %copy-start.8 = (f32[4,32,128]{2,1,0:T(8,128)}, f32[4,32,128]{2,1,0:T(8,128)S(1)}, u32[]{:S(2)}) copy-start(f32[4,32,128]{2,1,0:T(8,128)S(1)} %collective-permute-done.4.b0) | copy-start | bytes 196612
  249.4 6.4 %copy-start.10 = (f32[4,32,128]{2,1,0:T(8,128)}, f32[4,32,128]{2,1,0:T(8,128)S(1)}, u32[]{:S(2)}) copy-start(f32[4,32,128]{2,1,0:T(8,128)S(1)} %collective-permute-done.5.b1) | copy-start | bytes 196612
  249.7 6.1 %copy-start.11 = (f32[4,32,128]{2,1,0:T(8,128)}, f32[4,32,128]{2,1,0:T(8,128)S(1)}, u32[]{:S(2)}) copy-start(f32[4,32,128]{2,1,0:T(8,128)S(1)} %collective-permute-done.6.b3) | copy-start | bytes 196612
  255.8 0.6 copy-start.12
  287.8 19.0 %copy-start.3 = (f32[4,32,128]{2,1,0:T(8,128)}, f32[4,32,128]{2,1,0:T(8,128)S(1)}, u32[]{:S(2)}) copy-start(f32[4,32,128]{2,1,0:T(8,128)S(1)} %copy.23.b2) | copy-start | bytes 196612
  287.8 19.0 %collective-permute-start.10 = (f32[4,32,128]{2,1,0:T(8,128)S(1)}, f32[4,32,128]{2,1,0:T(8,128)S(1)}, u32[]{:S(2)}, u32[]{:S(2)}) collective-permute-start(f32[4,32,128]{2,1,0:T(8,128)S(1)} %copy.23.b2), channel_id=1, source_target_pairs={{4,0},{8,4},{12,8},{16,12},{20,16},{24,20},{28,24},{32,28},{36,32}... | collective-permute-start | bytes 196616 | tf_op jit(solution)/shard_map/ppermute | solution.py:530
  289.7 17.1 %collective-permute-start.11 = (f32[4,32,128]{2,1,0:T(8,128)S(1)}, f32[4,32,128]{2,1,0:T(8,128)S(1)}, u32[]{:S(2)}, u32[]{:S(2)}) collective-permute-start(f32[4,32,128]{2,1,0:T(8,128)S(1)} %copy.23.b2), channel_id=1, source_target_pairs={{8,0},{12,4},{16,8},{20,12},{24,16},{28,20},{32,24},{36,28},{40,32... | collective-permute-start | bytes 196616 | tf_op jit(solution)/shard_map/ppermute | solution.py:530
  291.6 15.2 %collective-permute-start.8 = (f32[4,32,128]{2,1,0:T(8,128)S(1)}, f32[4,32,128]{2,1,0:T(8,128)S(1)}, u32[]{:S(2)}, u32[]{:S(2)}) collective-permute-start(f32[4,32,128]{2,1,0:T(8,128)S(1)} %copy.23.b2), channel_id=1, source_target_pairs={{0,8},{4,12},{8,16},{12,20},{16,24},{20,28},{24,32},{28,36},{32,40... | collective-permute-start | bytes 196616 | tf_op jit(solution)/shard_map/ppermute | solution.py:530
  299.2 7.7 %collective-permute-start.9 = (f32[4,32,128]{2,1,0:T(8,128)S(1)}, f32[4,32,128]{2,1,0:T(8,128)S(1)}, u32[]{:S(2)}, u32[]{:S(2)}) collective-permute-start(f32[4,32,128]{2,1,0:T(8,128)S(1)} %copy.23.b2), channel_id=1, source_target_pairs={{0,4},{4,8},{8,12},{12,16},{16,20},{20,24},{24,28},{28,32},{32,36}... | collective-permute-start | bytes 196616 | tf_op jit(solution)/shard_map/ppermute | solution.py:530
  306.8 0.6 copy-start.5
  306.8 0.6 copy-start.6
  306.8 0.6 copy-start.7
  306.8 0.7 copy-start.9

commit v3 on v2

--- a/solution.py
+++ b/solution.py
@@ -168,25 +168,26 @@
 
 VMEM = pl.BlockSpec(memory_space=pltpu.VMEM)
 SMEM = pl.BlockSpec(memory_space=pltpu.SMEM)
-PARAMS = pltpu.CompilerParams(vmem_limit_bytes=56 * 1024 * 1024)
+BIG = 56 * 1024 * 1024
+SMALL = 32 * 1024 * 1024
 INTERPRET = False
 
 
-def call(body, name, ins, shape, scratch=()):
+def call(body, name, ins, shape, scratch=(), limit=SMALL):
     return pl.pallas_call(
         body,
         name=name,
         in_specs=ins,
         out_specs=VMEM,
-        out_shape=jax.ShapeDtypeStruct(shape, F32),
+        out_shape=shape,
         scratch_shapes=list(scratch),
-        compiler_params=PARAMS,
+        compiler_params=pltpu.CompilerParams(vmem_limit_bytes=limit),
         interpret=INTERPRET,
     )
 
 
 def forward(offsets, mass, fine, high, low, pairs):
-    return call(forward_kernel, "forward", [SMEM] + [VMEM] * 5, (NP * FORE, LANES), [pltpu.VMEM((64, LANES), F32)])(
+    return call(forward_kernel, "forward", [SMEM] + [VMEM] * 5, shaped(NP * FORE, LANES), [pltpu.VMEM((64, LANES), F32)], BIG)(
         offsets, mass, fine, high, low, pairs
     )
 
@@ -196,22 +197,24 @@
         plane_kernel,
         "plane",
         [SMEM, SMEM] + [VMEM] * 5,
-        (NP * BACK, LANES),
+        shaped(NP * BACK, LANES),
         [pltpu.VMEM((NP, LANES), F32)] * 4 + [pltpu.VMEM((SX + 8, LANES), F32)],
+        BIG,
     )(offsets, wave, got, high, low, column, row)
 
 
 def near_back(offsets, got, high, low):
-    return call(near_kernel, "near", [SMEM] + [VMEM] * 3, (256, LANES))(offsets, got, high, low)
+    return call(near_kernel, "near", [SMEM] + [VMEM] * 3, shaped(256, LANES))(offsets, got, high, low)
 
 
 def whole_back(got, high, low):
-    return call(whole_kernel, "whole", [VMEM] * 3, (NP, NP))(got, high, low)
+    return call(whole_kernel, "whole", [VMEM] * 3, shaped(NP, NP))(got, high, low)
 
 
 def swap(piece, lanes):
     piece = piece.reshape(NP, 1, lanes)
-    return lax.all_to_all(piece, ALL, 0, 0, tiled=True).reshape(NP * lanes // LANES, LANES)
+    piece = lax.all_to_all(piece, ALL, 0, 0, tiled=True).reshape(NP * lanes // LANES, LANES)
+    return pltpu.with_memory_space_constraint(piece, pltpu.VMEM)
 
 
 def constants():
@@ -496,7 +499,7 @@
     ]
 
 
-def many(body, name, count, shapes, scratch):
+def many(body, name, count, shapes, scratch, limit=SMALL):
     return pl.pallas_call(
         body,
         name=name,
@@ -504,7 +507,7 @@
         out_specs=[VMEM] * len(shapes),
         out_shape=shapes,
         scratch_shapes=scratch,
-        compiler_params=PARAMS,
+        compiler_params=pltpu.CompilerParams(vmem_limit_bytes=limit),
         interpret=INTERPRET,
     )
 
@@ -536,15 +539,19 @@
     every = jnp.pad(every, ((4, 4), (0, 0), (0, 0)))
     window = lax.dynamic_slice(every, (place, 0, 0), (9, 16, LANES))
     block = window.reshape(9, 4, 4, LANES).transpose(1, 0, 2, 3).reshape(4, 36, LANES)[:, 2:34]
-    return [block if step == 0 else shifted(block, "gx", GX, step) for step in (2, 1, 0, -1, -2)]
-
-
-def widened(fine):
+    blocks = [block if step == 0 else shifted(block, "gx", GX, step) for step in (2, 1, 0, -1, -2)]
+    return [pltpu.with_memory_space_constraint(block, pltpu.VMEM) for block in blocks]
+
+
+def taller(fine):
     sides = ("group", "gy")
-    tall = jnp.concatenate([shifted(fine, sides, YY, 1), fine, shifted(fine, sides, YY, -1)], axis=1)
+    return jnp.concatenate([shifted(fine, sides, YY, 1), fine, shifted(fine, sides, YY, -1)], axis=1)
+
+
+def wider(tall):
     before = shifted(tall[8:16], "gx", GX, 1)
     behind = shifted(tall[0:8], "gx", GX, -1)
-    return jnp.concatenate([before, tall, behind], axis=0)
+    return pltpu.with_memory_space_constraint(jnp.concatenate([before, tall, behind], axis=0), pltpu.VMEM)
 
 
 def local(parent_mass, fine_mass, offsets):
@@ -556,8 +563,10 @@
     tables = (pairs, spread, jnp.asarray(merge, BF16), jnp.asarray(merge.T, BF16))
     pos = jnp.stack([lax.axis_index("gx"), lax.axis_index(("group", "gy"))]).astype(jnp.int32)
     wave = lax.dynamic_slice(eigen, (lax.axis_index(ALL),), (1,))
-    wide = widened(fine_mass)
+    tall = taller(fine_mass)
     got = swap(forward(offsets, parent_mass.reshape(NP, NP), fine_mass, high, low, pairs), FORE * LANES)
+    got, tall = lax.optimization_barrier((got, tall))
+    wide = wider(tall)
     got = swap(spectral(offsets, wave, got, high, low, column, row), BACK * LANES)
     near = near_back(offsets, got, high, low)
     start, resid, corr, lower = opening(pos, near, wide, pairs, spread)

time: 316 us -> 299 us (0.946)
  the two profiles are of different devices: /device:TPU:112 before, /device:TPU:128 now
where the time goes in v3:
time: 299 us
  waiting for transfers between devices  151 us (51%)
  starting transfers between devices  87.2 us (29%)
  Pallas kernels  36.2 us (12%)
  blocking collectives  18.7 us (6%)
  local copies, waits for them, and re-layouts  4.5 us (2%)
    ppermute x12, waiting for transfers between devices, shifted(): lax.ppermute(value, axes, [(i, i + step) for i in range(size) if 0 <= i +...  71.3 us
    all_to_all x2, waiting for transfers between devices, swap(): lax.all_to_all(piece, ALL, 0, 0, tiled=True)  61.3 us
    ppermute x12, starting transfers between devices, shifted(): lax.ppermute(value, axes, [(i, i + step) for i in range(size) if 0 <= i +...  42.5 us
    all_to_all x2, starting transfers between devices, swap(): lax.all_to_all(piece, ALL, 0, 0, tiled=True)  37.1 us
    all_to_all x1, blocking collectives, gather(): every = lax.all_to_all(every, ('group', 'gy'), 0, 0, tiled=True)  18.7 us
    all_to_all x1, waiting for transfers between devices, gather(): every = lax.all_to_all(every, ('group', 'gy'), 0, 0, tiled=True)  18.3 us
    pallas_call x1, Pallas kernels, spectral(): call(plane_kernel, 'plane', [SMEM, SMEM] + [VMEM] * 5, shaped(NP * BACK,...  10.6 us
    pallas_call x1, Pallas kernels, turning(): many(turn_kernel, 'turning', 11, shapes, inner() + [held(64, LANES)])  8.63 us
  transfers between devices with their start and end apart: 15, of which 8 were waited for; matrix products, arithmetic and copies ran while one was open for 0% of the time, Pallas kernels for 1%

profile of v3, /device:TPU:128, one launch (start us, length us, event | category | flops | bytes accessed | tf_op | source)
XLA Modules:
  0.0 298.5 jit_solution(10485132706961701049)
XLA Ops:
  0.6 4.1 %forward.1 = f32[2560,128]{1,0:T(8,128)} custom-call(s32[3]{0:T(128)} %offsets.5, f32[512,512]{1,0:T(8,128)} %bitcast.22, f32[16,8,128]{2,1,0:T(8,128)} %fine.1, bf16[512,512]{1,0:T(8,128)(2,1)} %constant.54.high, bf16[512,512]{1,0:T(8,128)(2,1)} %constant.57.low, bf16[128,128]{1,0:T(8,128)(2,1)} %constant.42.clone.pairs), custom_call_target="tpu_custom_call" | custom-call | tf_op jit(solution)/shard_map/forward/pallas_call | solution.py:190
  4.7 22.5 %all-to-all-start = ((f32[512,1,640]{2,1,0:T(1,128)}), f32[512,1,640]{2,1,0:T(1,128)S(1)}, u32[]{:S(2)}, u32[]{:S(2)}) async-start(f32[512,1,640]{2,1,0:T(1,128)} %bitcast.20), calls=%async_computation | async-start | bytes 2621440 | tf_op jit(solution)/shard_map/all_to_all | solution.py:216
  27.2 3.4 %collective-permute-start = (f32[16,8,128]{2,1,0:T(8,128)S(1)}, f32[16,8,128]{2,1,0:T(8,128)S(1)}, u32[]{:S(2)}, u32[]{:S(2)}) collective-permute-start(f32[16,8,128]{2,1,0:T(8,128)S(1)} %copy-done.11), channel_id=1, source_target_pairs={{0,1},{1,2},{2,3},{3,128},{128,129},{129,130},{130,131},{131,256},... | collective-permute-start | bytes 196616 | tf_op jit(solution)/shard_map/ppermute | solution.py:533
  30.6 1.3 collective-permute-start.1
  31.9 1.3 dynamic_slice.9.wave
  33.2 0.0 collective-permute-done
  33.2 3.8 %collective-permute-done.1 = f32[16,8,128]{2,1,0:T(8,128)S(1)} collective-permute-done((f32[16,8,128]{2,1,0:T(8,128)S(1)}, f32[16,8,128]{2,1,0:T(8,128)S(1)}, u32[]{:S(2)}, u32[]{:S(2)}) %collective-permute-start.1) | collective-permute-done | bytes 65568 | tf_op jit(solution)/shard_map/ppermute | solution.py:533
  37.1 53.7 %all-to-all-done = f32[512,1,640]{2,1,0:T(1,128)S(1)} async-done(((f32[512,1,640]{2,1,0:T(1,128)}), f32[512,1,640]{2,1,0:T(1,128)S(1)}, u32[]{:S(2)}, u32[]{:S(2)}) %all-to-all-start) | async-done | bytes 1310752 | tf_op jit(solution)/shard_map/all_to_all | solution.py:216
  90.8 10.6 %plane.1 = f32[3072,128]{1,0:T(8,128)} custom-call(s32[3]{0:T(128)} %offsets.5, f32[1]{0:T(128)} %dynamic_slice.9.wave, f32[2560,128]{1,0:T(8,128)S(1)} %bitcast.18, bf16[512,512]{1,0:T(8,128)(2,1)} %constant.54.high, bf16[512,512]{1,0:T(8,128)(2,1)} %constant.57.low, f32[512,1]{1,0:T(8,128)} %constant.43.clone.column, f32[1,512]{1,0:T(1,128)} %constant.44.clone.row), custom_call_target="tpu_custom_call" | custom-call | tf_op jit(solution)/shard_map/plane/pallas_call | solution.py:196
  101.3 14.7 %all-to-all-start.1 = ((f32[512,1,768]{2,1,0:T(1,128)}), f32[512,1,768]{2,1,0:T(1,128)S(1)}, u32[]{:S(2)}, u32[]{:S(2)}) async-start(f32[512,1,768]{2,1,0:T(1,128)} %bitcast.19), calls=%async_computation.1 | async-start | bytes 3145728 | tf_op jit(solution)/shard_map/all_to_all | solution.py:216
  116.0 3.4 %collective-permute-start.2 = (f32[8,24,128]{2,1,0:T(8,128)S(1)}, f32[8,24,128]{2,1,0:T(8,128)S(1)}, u32[]{:S(2)}, u32[]{:S(2)}) collective-permute-start(f32[8,24,128]{2,1,0:T(8,128)S(1)} %get-tuple-element.18), channel_id=1, source_target_pairs={{0,4},{4,8},{8,12},{12,16},{16,20},{20,24},{24,28},{28,32},{32,36}... | collective-permute-start | bytes 294920 | tf_op jit(solution)/shard_map/ppermute | solution.py:533
  119.5 5.7 %collective-permute-start.3 = (f32[8,24,128]{2,1,0:T(8,128)S(1)}, f32[8,24,128]{2,1,0:T(8,128)S(1)}, u32[]{:S(2)}, u32[]{:S(2)}) collective-permute-start(f32[8,24,128]{2,1,0:T(8,128)S(1)} %get-tuple-element.19), channel_id=1, source_target_pairs={{4,0},{8,4},{12,8},{16,12},{20,16},{24,20},{28,24},{32,28},{36,32}... | collective-permute-start | bytes 294920 | tf_op jit(solution)/shard_map/ppermute | solution.py:533
  125.2 0.1 pad_add_fusion.pos
  125.3 58.5 %collective-permute-done.2 = f32[8,24,128]{2,1,0:T(8,128)S(1)} collective-permute-done((f32[8,24,128]{2,1,0:T(8,128)S(1)}, f32[8,24,128]{2,1,0:T(8,128)S(1)}, u32[]{:S(2)}, u32[]{:S(2)}) %collective-permute-start.2) | collective-permute-done | bytes 98336 | tf_op jit(solution)/shard_map/ppermute | solution.py:533
  183.8 0.0 collective-permute-done.3
  183.8 0.0 copy-start.4
  183.8 0.0 copy-start.5
  183.8 7.6 %all-to-all-done.1 = f32[512,1,768]{2,1,0:T(1,128)S(1)} async-done(((f32[512,1,768]{2,1,0:T(1,128)}), f32[512,1,768]{2,1,0:T(1,128)S(1)}, u32[]{:S(2)}, u32[]{:S(2)}) %all-to-all-start.1) | async-done | bytes 1572896 | tf_op jit(solution)/shard_map/all_to_all | solution.py:216
  191.4 0.0 copy-start.6
  191.5 0.0 copy-start.7
  191.5 1.3 near.1
  192.8 2.8 opening.1
  195.5 0.8 copy-done.2
  196.3 0.6 copy-done.8
  196.9 0.7 broadcast_in_dim.4
  197.6 7.6 %all-to-all-start.2 = ((f32[16,16,128]{2,1,0:T(8,128)}), f32[16,16,128]{2,1,0:T(8,128)S(1)}, u32[]{:S(2)}, u32[]{:S(2)}) async-start(f32[16,16,128]{2,1,0:T(8,128)} %broadcast_in_dim.4), calls=%async_computation.2 | async-start | bytes 262144 | tf_op jit(solution)/shard_map/all_to_all | solution.py:538
  205.2 18.3 %all-to-all-done.2 = f32[16,16,128]{2,1,0:T(8,128)S(1)} async-done(((f32[16,16,128]{2,1,0:T(8,128)}), f32[16,16,128]{2,1,0:T(8,128)S(1)}, u32[]{:S(2)}, u32[]{:S(2)}) %all-to-all-start.2) | async-done | bytes 131104 | tf_op jit(solution)/shard_map/all_to_all | solution.py:538
  223.5 1.9 collective-permute-start.4
  225.5 1.9 collective-permute-start.5
  227.4 7.2 %collective-permute-start.6 = (f32[4,32,128]{2,1,0:T(8,128)S(1)}, f32[4,32,128]{2,1,0:T(8,128)S(1)}, u32[]{:S(2)}, u32[]{:S(2)}) collective-permute-start(f32[4,32,128]{2,1,0:T(8,128)S(1)} %copy.22.b2), channel_id=1, source_target_pairs={{4,0},{8,4},{12,8},{16,12},{20,16},{24,20},{28,24},{32,28},{36,32}... | collective-permute-start | bytes 196616 | tf_op jit(solution)/shard_map/ppermute | solution.py:533
  234.6 4.2 %collective-permute-start.7 = (f32[4,32,128]{2,1,0:T(8,128)S(1)}, f32[4,32,128]{2,1,0:T(8,128)S(1)}, u32[]{:S(2)}, u32[]{:S(2)}) collective-permute-start(f32[4,32,128]{2,1,0:T(8,128)S(1)} %copy.22.b2), channel_id=1, source_target_pairs={{8,0},{12,4},{16,8},{20,12},{24,16},{28,20},{32,24},{36,28},{40,32... | collective-permute-start | bytes 196616 | tf_op jit(solution)/shard_map/ppermute | solution.py:533
  238.9 0.0 collective-permute-done.4.b0
  238.9 0.0 collective-permute-done.5.b1
  238.9 0.0 collective-permute-done.6.b3
  238.9 3.4 %collective-permute-done.7.b4 = f32[4,32,128]{2,1,0:T(8,128)S(1)} collective-permute-done((f32[4,32,128]{2,1,0:T(8,128)S(1)}, f32[4,32,128]{2,1,0:T(8,128)S(1)}, u32[]{:S(2)}, u32[]{:S(2)}) %collective-permute-start.7) | collective-permute-done | bytes 65568 | tf_op jit(solution)/shard_map/ppermute | solution.py:533
  242.3 1.0 copy-done.3
  243.3 8.6 %turning.1 = (f32[32,24,128]{2,1,0:T(8,128)S(1)}, f32[16,128]{1,0:T(8,128)S(1)}) custom-call(s32[2]{0:T(128)S(1)} %pad_add_fusion.pos, f32[4,32,128]{2,1,0:T(8,128)S(1)} %collective-permute-done.4.b0, f32[4,32,128]{2,1,0:T(8,128)S(1)} %collective-permute-done.5.b1, f32[4,32,128]{2,1,0:T(8,128)S(1)} %copy.22.b2, f32[4,32,128]{2,1,0:T(8,128)S(1)} %collective-permute-done.6.b3, ...), custom_call_target="tpu_custom_call" | custom-call | tf_op jit(solution)/shard_map/turning/pallas_call | solution.py:523
  252.0 18.7 %all_to_all.20 = f32[16,16,128]{2,1,0:T(8,128)S(1)} all-to-all(f32[16,16,128]{2,1,0:T(8,128)S(1)} %broadcast_in_dim.5), channel_id=1, replica_groups=mesh['group'=4,'gx'=32,'gy'=4] {'group','gy'}, dimensions={0} | all-to-all | bytes 262144 | tf_op jit(solution)/shard_map/all_to_all | solution.py:538
  270.7 0.0 copy-start.9
  270.7 4.1 %collective-permute-start.10 = (f32[4,32,128]{2,1,0:T(8,128)S(1)}, f32[4,32,128]{2,1,0:T(8,128)S(1)}, u32[]{:S(2)}, u32[]{:S(2)}) collective-permute-start(f32[4,32,128]{2,1,0:T(8,128)S(1)} %copy.23.b2), channel_id=1, source_target_pairs={{4,0},{8,4},{12,8},{16,12},{20,16},{24,20},{28,24},{32,28},{36,32}... | collective-permute-start | bytes 196616 | tf_op jit(solution)/shard_map/ppermute | solution.py:533
  274.8 3.3 %collective-permute-start.11 = (f32[4,32,128]{2,1,0:T(8,128)S(1)}, f32[4,32,128]{2,1,0:T(8,128)S(1)}, u32[]{:S(2)}, u32[]{:S(2)}) collective-permute-start(f32[4,32,128]{2,1,0:T(8,128)S(1)} %copy.23.b2), channel_id=1, source_target_pairs={{8,0},{12,4},{16,8},{20,12},{24,16},{28,20},{32,24},{36,28},{40,32... | collective-permute-start | bytes 196616 | tf_op jit(solution)/shard_map/ppermute | solution.py:533
  278.1 4.0 %collective-permute-start.8 = (f32[4,32,128]{2,1,0:T(8,128)S(1)}, f32[4,32,128]{2,1,0:T(8,128)S(1)}, u32[]{:S(2)}, u32[]{:S(2)}) collective-permute-start(f32[4,32,128]{2,1,0:T(8,128)S(1)} %copy.23.b2), channel_id=1, source_target_pairs={{0,8},{4,12},{8,16},{12,20},{16,24},{20,28},{24,32},{28,36},{32,40... | collective-permute-start | bytes 196616 | tf_op jit(solution)/shard_map/ppermute | solution.py:533
  282.2 1.9 collective-permute-start.9
  284.1 2.0 whole.1
  286.1 0.0 collective-permute-done.10.b3
  286.1 1.9 collective-permute-done.8.b0
  288.0 3.6 %collective-permute-done.9.b1 = f32[4,32,128]{2,1,0:T(8,128)S(1)} collective-permute-done((f32[4,32,128]{2,1,0:T(8,128)S(1)}, f32[4,32,128]{2,1,0:T(8,128)S(1)}, u32[]{:S(2)}, u32[]{:S(2)}) %collective-permute-start.9) | collective-permute-done | bytes 65568 | tf_op jit(solution)/shard_map/ppermute | solution.py:533
  291.6 6.9 %closing.1 = f32[16,8,128]{2,1,0:T(8,128)} custom-call(s32[2]{0:T(128)S(1)} %pad_add_fusion.pos, f32[4,32,128]{2,1,0:T(8,128)S(1)} %collective-permute-done.8.b0, f32[4,32,128]{2,1,0:T(8,128)S(1)} %collective-permute-done.9.b1, f32[4,32,128]{2,1,0:T(8,128)S(1)} %copy.23.b2, f32[4,32,128]{2,1,0:T(8,128)S(1)} %collective-permute-done.10.b3, ...), custom_call_target="tpu_custom_call" | custom-call | tf_op jit(solution)/shard_map/closing/pallas_call | solution.py:527
  (29 shorter events, 0.2 us)
Async XLA Ops:
  4.7 22.5 %copy-start.11 = (f32[16,8,128]{2,1,0:T(8,128)S(1)}, f32[16,8,128]{2,1,0:T(8,128)}, u32[]{:S(2)}) copy-start(f32[16,8,128]{2,1,0:T(8,128)} %fine.1) | copy-start | bytes 196612
  4.7 86.1 %all-to-all-start = ((f32[512,1,640]{2,1,0:T(1,128)}), f32[512,1,640]{2,1,0:T(1,128)S(1)}, u32[]{:S(2)}, u32[]{:S(2)}) async-start(f32[512,1,640]{2,1,0:T(1,128)} %bitcast.20), calls=%async_computation | async-start | bytes 2621440 | tf_op jit(solution)/shard_map/all_to_all | solution.py:216
  27.2 6.0 %collective-permute-start = (f32[16,8,128]{2,1,0:T(8,128)S(1)}, f32[16,8,128]{2,1,0:T(8,128)S(1)}, u32[]{:S(2)}, u32[]{:S(2)}) collective-permute-start(f32[16,8,128]{2,1,0:T(8,128)S(1)} %copy-done.11), channel_id=1, source_target_pairs={{0,1},{1,2},{2,3},{3,128},{128,129},{129,130},{130,131},{131,256},... | collective-permute-start | bytes 196616 | tf_op jit(solution)/shard_map/ppermute | solution.py:533
  30.6 6.4 %collective-permute-start.1 = (f32[16,8,128]{2,1,0:T(8,128)S(1)}, f32[16,8,128]{2,1,0:T(8,128)S(1)}, u32[]{:S(2)}, u32[]{:S(2)}) collective-permute-start(f32[16,8,128]{2,1,0:T(8,128)S(1)} %copy-done.11), channel_id=1, source_target_pairs={{1,0},{2,1},{3,2},{128,3},{129,128},{130,129},{131,130},{256,131},... | collective-permute-start | bytes 196616 | tf_op jit(solution)/shard_map/ppermute | solution.py:533
  101.3 90.1 %copy-start = (bf16[512,512]{1,0:T(8,128)(2,1)S(1)}, bf16[512,512]{1,0:T(8,128)(2,1)}, u32[]{:S(2)}) copy-start(bf16[512,512]{1,0:T(8,128)(2,1)} %constant.54.high) | copy-start | bytes 1572868
  101.3 90.1 %copy-start.1 = (bf16[512,512]{1,0:T(8,128)(2,1)S(1)}, bf16[512,512]{1,0:T(8,128)(2,1)}, u32[]{:S(2)}) copy-start(bf16[512,512]{1,0:T(8,128)(2,1)} %constant.57.low) | copy-start | bytes 1572868
  101.3 90.1 %copy-start.10 = (s32[3]{0:T(128)S(1)}, s32[3]{0:T(128)}, u32[]{:S(2)}) copy-start(s32[3]{0:T(128)} %offsets.5) | copy-start | bytes 40
  101.3 90.1 %all-to-all-start.1 = ((f32[512,1,768]{2,1,0:T(1,128)}), f32[512,1,768]{2,1,0:T(1,128)S(1)}, u32[]{:S(2)}, u32[]{:S(2)}) async-start(f32[512,1,768]{2,1,0:T(1,128)} %bitcast.19), calls=%async_computation.1 | async-start | bytes 3145728 | tf_op jit(solution)/shard_map/all_to_all | solution.py:216
  116.0 67.7 %collective-permute-start.2 = (f32[8,24,128]{2,1,0:T(8,128)S(1)}, f32[8,24,128]{2,1,0:T(8,128)S(1)}, u32[]{:S(2)}, u32[]{:S(2)}) collective-permute-start(f32[8,24,128]{2,1,0:T(8,128)S(1)} %get-tuple-element.18), channel_id=1, source_target_pairs={{0,4},{4,8},{8,12},{12,16},{16,20},{20,24},{24,28},{28,32},{32,36}... | collective-permute-start | bytes 294920 | tf_op jit(solution)/shard_map/ppermute | solution.py:533
  119.5 64.3 %collective-permute-start.3 = (f32[8,24,128]{2,1,0:T(8,128)S(1)}, f32[8,24,128]{2,1,0:T(8,128)S(1)}, u32[]{:S(2)}, u32[]{:S(2)}) collective-permute-start(f32[8,24,128]{2,1,0:T(8,128)S(1)} %get-tuple-element.19), channel_id=1, source_target_pairs={{4,0},{8,4},{12,8},{16,12},{20,16},{24,20},{28,24},{32,28},{36,32}... | collective-permute-start | bytes 294920 | tf_op jit(solution)/shard_map/ppermute | solution.py:533
  183.8 8.9 %copy-start.4 = (bf16[128,128]{1,0:T(8,128)(2,1)S(1)}, bf16[128,128]{1,0:T(8,128)(2,1)}, u32[]{:S(2)}) copy-start(bf16[128,128]{1,0:T(8,128)(2,1)} %constant.42.clone.pairs) | copy-start | bytes 98308
  183.8 8.9 %copy-start.5 = (bf16[128,128]{1,0:T(8,128)(2,1)S(1)}, bf16[128,128]{1,0:T(8,128)(2,1)}, u32[]{:S(2)}) copy-start(bf16[128,128]{1,0:T(8,128)(2,1)} %constant.58.spread) | copy-start | bytes 98308
  191.4 50.9 %copy-start.6 = (bf16[128,128]{1,0:T(8,128)(2,1)S(1)}, bf16[128,128]{1,0:T(8,128)(2,1)}, u32[]{:S(2)}) copy-start(bf16[128,128]{1,0:T(8,128)(2,1)} %constant.46.clone.merge) | copy-start | bytes 98308
  191.5 50.9 %copy-start.7 = (bf16[128,128]{1,0:T(8,128)(2,1)S(1)}, bf16[128,128]{1,0:T(8,128)(2,1)}, u32[]{:S(2)}) copy-start(bf16[128,128]{1,0:T(8,128)(2,1)} %constant.47.clone.widen) | copy-start | bytes 98308
  195.5 0.8 copy-start.2
  196.3 0.6 copy-start.8
  197.6 25.9 %all-to-all-start.2 = ((f32[16,16,128]{2,1,0:T(8,128)}), f32[16,16,128]{2,1,0:T(8,128)S(1)}, u32[]{:S(2)}, u32[]{:S(2)}) async-start(f32[16,16,128]{2,1,0:T(8,128)} %broadcast_in_dim.4), calls=%async_computation.2 | async-start | bytes 262144 | tf_op jit(solution)/shard_map/all_to_all | solution.py:538
  223.5 15.3 %collective-permute-start.4 = (f32[4,32,128]{2,1,0:T(8,128)S(1)}, f32[4,32,128]{2,1,0:T(8,128)S(1)}, u32[]{:S(2)}, u32[]{:S(2)}) collective-permute-start(f32[4,32,128]{2,1,0:T(8,128)S(1)} %copy.22.b2), channel_id=1, source_target_pairs={{0,8},{4,12},{8,16},{12,20},{16,24},{20,28},{24,32},{28,36},{32,40... | collective-permute-start | bytes 196616 | tf_op jit(solution)/shard_map/ppermute | solution.py:533
  225.5 13.4 %collective-permute-start.5 = (f32[4,32,128]{2,1,0:T(8,128)S(1)}, f32[4,32,128]{2,1,0:T(8,128)S(1)}, u32[]{:S(2)}, u32[]{:S(2)}) collective-permute-start(f32[4,32,128]{2,1,0:T(8,128)S(1)} %copy.22.b2), channel_id=1, source_target_pairs={{0,4},{4,8},{8,12},{12,16},{16,20},{20,24},{24,28},{28,32},{32,36}... | collective-permute-start | bytes 196616 | tf_op jit(solution)/shard_map/ppermute | solution.py:533
  227.4 11.5 %collective-permute-start.6 = (f32[4,32,128]{2,1,0:T(8,128)S(1)}, f32[4,32,128]{2,1,0:T(8,128)S(1)}, u32[]{:S(2)}, u32[]{:S(2)}) collective-permute-start(f32[4,32,128]{2,1,0:T(8,128)S(1)} %copy.22.b2), channel_id=1, source_target_pairs={{4,0},{8,4},{12,8},{16,12},{20,16},{24,20},{28,24},{32,28},{36,32}... | collective-permute-start | bytes 196616 | tf_op jit(solution)/shard_map/ppermute | solution.py:533
  234.6 7.7 %collective-permute-start.7 = (f32[4,32,128]{2,1,0:T(8,128)S(1)}, f32[4,32,128]{2,1,0:T(8,128)S(1)}, u32[]{:S(2)}, u32[]{:S(2)}) collective-permute-start(f32[4,32,128]{2,1,0:T(8,128)S(1)} %copy.22.b2), channel_id=1, source_target_pairs={{8,0},{12,4},{16,8},{20,12},{24,16},{28,20},{32,24},{36,28},{40,32... | collective-permute-start | bytes 196616 | tf_op jit(solution)/shard_map/ppermute | solution.py:533
  242.3 1.0 copy-start.3
  270.7 21.0 %copy-start.9 = (f32[16,8,128]{2,1,0:T(8,128)S(1)}, f32[16,8,128]{2,1,0:T(8,128)}, u32[]{:S(2)}) copy-start(f32[16,8,128]{2,1,0:T(8,128)} %copy-done.8) | copy-start | bytes 196612
  270.7 15.4 %collective-permute-start.10 = (f32[4,32,128]{2,1,0:T(8,128)S(1)}, f32[4,32,128]{2,1,0:T(8,128)S(1)}, u32[]{:S(2)}, u32[]{:S(2)}) collective-permute-start(f32[4,32,128]{2,1,0:T(8,128)S(1)} %copy.23.b2), channel_id=1, source_target_pairs={{4,0},{8,4},{12,8},{16,12},{20,16},{24,20},{28,24},{32,28},{36,32}... | collective-permute-start | bytes 196616 | tf_op jit(solution)/shard_map/ppermute | solution.py:533
  274.8 11.3 %collective-permute-start.11 = (f32[4,32,128]{2,1,0:T(8,128)S(1)}, f32[4,32,128]{2,1,0:T(8,128)S(1)}, u32[]{:S(2)}, u32[]{:S(2)}) collective-permute-start(f32[4,32,128]{2,1,0:T(8,128)S(1)} %copy.23.b2), channel_id=1, source_target_pairs={{8,0},{12,4},{16,8},{20,12},{24,16},{28,20},{32,24},{36,28},{40,32... | collective-permute-start | bytes 196616 | tf_op jit(solution)/shard_map/ppermute | solution.py:533
  278.1 9.9 %collective-permute-start.8 = (f32[4,32,128]{2,1,0:T(8,128)S(1)}, f32[4,32,128]{2,1,0:T(8,128)S(1)}, u32[]{:S(2)}, u32[]{:S(2)}) collective-permute-start(f32[4,32,128]{2,1,0:T(8,128)S(1)} %copy.23.b2), channel_id=1, source_target_pairs={{0,8},{4,12},{8,16},{12,20},{16,24},{20,28},{24,32},{28,36},{32,40... | collective-permute-start | bytes 196616 | tf_op jit(solution)/shard_map/ppermute | solution.py:533
  282.2 9.5 %collective-permute-start.9 = (f32[4,32,128]{2,1,0:T(8,128)S(1)}, f32[4,32,128]{2,1,0:T(8,128)S(1)}, u32[]{:S(2)}, u32[]{:S(2)}) collective-permute-start(f32[4,32,128]{2,1,0:T(8,128)S(1)} %copy.23.b2), channel_id=1, source_target_pairs={{0,4},{4,8},{8,12},{12,16},{16,20},{20,24},{24,28},{28,32},{32,36}... | collective-permute-start | bytes 196616 | tf_op jit(solution)/shard_map/ppermute | solution.py:533
